TPU v7x, 512 devices: a whole 4x8x8 slice. The times are simulated.
512 devices in a mesh: slab: 128 (over z, x, y_hi, core), tm: 4 (over y_lo).
Axes of the slice: x: 4, y: 8 (y_hi: 2, y_lo: 4; y = y_hi * 4 + y_lo), z: 8, core: 2. Of those that a mesh axis runs over, the one named last changes fastest.
Arguments:
- field: float32 [2, 128, 256, 512], P(None, 'slab', None, 'tm'), may hold values from -110 to 110
Outputs:
- evolved: float32 [2, 128, 256, 512], P(None, 'slab', None, 'tm')
All inputs are finite; a program needn't handle non-finite values.
Results may differ from a plain program's by a relative error of at most 0.000098.
Values sent between devices are 32-bit elements; how exact they have to be, the bound alone decides.
No kernel may reach another device: no remote copies, remote signals or barrier semaphores. Data moves between devices by JAX's collectives and lax.ppermute only.
A program may use at most 64 MiB of HBM per device.

v0:
```python
import math

import jax
import jax.numpy as jnp
import ml_dtypes
import numpy as np
from jax import lax
from jax.experimental import pallas as pl
from jax.experimental.pallas import tpu as pltpu
from jax.sharding import Mesh
from jax.sharding import PartitionSpec as P

NX = 128
NY = 256
NT = 512
SLAB = ("z", "x", "h", "c")
CHIPS = ("z", "x", "h", "t")

TWO_PI = 2.0 * math.pi
DIFFRACT = 4.0
DISPERSE = 3.0
KERR = 0.05
WELL = 1.5
EPSILON = 1e-06


def propagator(length, weight):
    positions = np.arange(length)
    signed = np.where(2 * positions < length, positions, positions - length)
    angle = weight * (signed * (TWO_PI / length)) ** 2
    kernel = np.fft.ifft(np.exp(1j * angle))
    return kernel[(positions[:, None] - positions[None, :]) % length]


def well_phase(length):
    place = (np.arange(length) - (length - 1) / 2.0) / (length / 2.0)
    return np.exp(-1j * WELL * place**2)


def split(matrix):
    full = matrix.astype(np.float32)
    high = full.astype(ml_dtypes.bfloat16)
    low = (matrix - high.astype(np.float64)).astype(ml_dtypes.bfloat16)
    return np.stack([high, low])


def stacked_rows(matrix):
    return split(np.concatenate([matrix.real, matrix.imag], axis=0))


def real_block(matrix):
    return split(np.block([[matrix.real, -matrix.imag], [matrix.imag, matrix.real]]))


def pieces(value):
    high = value.astype(jnp.bfloat16)
    return high, (value - high.astype(jnp.float32)).astype(jnp.bfloat16)


def dot(left, right):
    return jnp.dot(left, right, preferred_element_type=jnp.float32)


def dot_table_left(table_ref, data):
    high, low = pieces(data)
    return dot(table_ref[0], high) + (dot(table_ref[0], low) + dot(table_ref[1], high))


def along_y(real, imag, table_ref):
    r = dot_table_left(table_ref, jnp.concatenate([real, imag], axis=1))
    return r[:NY, :128] - r[NY:, 128:], r[:NY, 128:] + r[NY:, :128]


def along_t(real, imag, table_ref):
    rows = real.shape[0]
    high, low = pieces(jnp.concatenate([real, imag], axis=0))
    both = jnp.concatenate([high, low], axis=0)

    def product(k):
        p = dot(both, table_ref[k, 0])
        return p[: 2 * rows] + (p[2 * rows :] + dot(high, table_ref[k, 1]))

    by_real = product(0)
    by_imag = product(1)
    return by_real[:rows] - by_imag[rows:], by_real[rows:] + by_imag[:rows]


def first_kernel(field_ref, table_ref, out_ref, power_ref):
    real = field_ref[0]
    imag = field_ref[1]
    out_real, out_imag = along_y(real, imag, table_ref)
    out_ref[pl.ds(0, NY, stride=2), :] = out_real
    out_ref[pl.ds(1, NY, stride=2), :] = out_imag
    power = jnp.sum(real * real + imag * imag, axis=0, keepdims=True)
    power_ref[...] = jnp.broadcast_to(power, power_ref.shape)


def time_kernel(core_ref, in_ref, table_ref, keep_ref, send_ref):
    def part(p):
        return jnp.concatenate([in_ref[pl.ds(2 * g + p, NX // 2, stride=8), :] for g in range(4)], axis=1)

    outs = along_t(part(0), part(1), table_ref)
    lower = core_ref[0] == 0
    half = NT // 2
    for p in range(2):
        keep_ref[p] = jnp.where(lower, outs[p][:, :half], outs[p][:, half:])
        send_ref[p] = jnp.where(lower, outs[p][:, half:], outs[p][:, :half])


def kick_kernel(core_ref, keep_in_ref, got_ref, power_ref, table_ref, table2_ref, keep_ref, send_ref):
    lower = core_ref[0] == 0
    rows = []
    for p in range(2):
        rows.append(jnp.where(lower, keep_in_ref[p], got_ref[p]))
        rows.append(jnp.where(lower, got_ref[p], keep_in_ref[p]))
    first = dot_table_left(table_ref, jnp.concatenate(rows, axis=0))
    total = jnp.sum(jnp.sum(power_ref[...], axis=0, keepdims=True), axis=1, keepdims=True)
    scale = 1.0 / jnp.sqrt(total * (1.0 / (NX * NY * NT)) + EPSILON)
    real = first[:NX] * scale
    imag = first[NX:] * scale
    angle = KERR * (real * real + imag * imag)
    cos_turn = jnp.cos(angle)
    sin_turn = jnp.sin(angle)
    kicked = jnp.concatenate([real * cos_turn - imag * sin_turn, real * sin_turn + imag * cos_turn], axis=0)
    second = dot_table_left(table2_ref, kicked)
    half = NX // 2
    for p in range(2):
        even = second[p * NX : p * NX + half]
        odd = second[p * NX + half : (p + 1) * NX]
        keep_ref[p] = jnp.where(lower, even, odd)
        send_ref[p] = jnp.where(lower, odd, even)


def time_back_kernel(core_ref, keep_in_ref, got_ref, table_ref, out_ref):
    lower = core_ref[0] == 0

    def part(p):
        kept = keep_in_ref[p]
        got = got_ref[p]
        return jnp.concatenate([jnp.where(lower, kept, got), jnp.where(lower, got, kept)], axis=1)

    outs = along_t(part(0), part(1), table_ref)
    for p in range(2):
        for g in range(4):
            out_ref[pl.ds(2 * g + p, NX // 2, stride=8), :] = outs[p][:, 128 * g : 128 * (g + 1)]


def last_kernel(in_ref, table_ref, out_ref):
    real = in_ref[pl.ds(0, NY, stride=2), :]
    imag = in_ref[pl.ds(1, NY, stride=2), :]
    out_real, out_imag = along_y(real, imag, table_ref)
    out_ref[0] = out_real
    out_ref[1] = out_imag


def call(kernel, shapes, *args):
    specs = [
        pl.BlockSpec(memory_space=pltpu.SMEM if a.dtype == jnp.int32 else pltpu.VMEM) for a in args
    ]
    outs = [jax.ShapeDtypeStruct(s, jnp.float32) for s in shapes]
    return pl.pallas_call(
        kernel,
        in_specs=specs,
        out_specs=[pl.BlockSpec(memory_space=pltpu.VMEM) for _ in outs],
        out_shape=outs,
        name=kernel.__name__,
    )(*args)


def to_chips(rows):
    moved = lax.all_to_all(rows.reshape(NY, 2, 128), CHIPS, split_axis=0, concat_axis=0, tiled=True)
    return moved.reshape(2 * NY, 128)


def swap(value):
    return lax.ppermute(value, "c", [(0, 1), (1, 0)])


def on_device(field, y_table, y_back, t_table, x_table, x_back):
    core = lax.axis_index("c").astype(jnp.int32).reshape(1)
    rows, power = call(first_kernel, [(2 * NY, 128), (32, 128)], field.reshape(2, NY, 128), y_table)
    moved = to_chips(rows)
    power = lax.all_to_all(power, ("z", "x"), split_axis=0, concat_axis=0, tiled=True)
    power = jnp.broadcast_to(jnp.sum(power, axis=0, keepdims=True), (16, 128))
    power = lax.all_to_all(power, ("h", "c", "t"), split_axis=0, concat_axis=0, tiled=True)
    half = (2, NX // 2, NT // 2)
    keep, send = call(time_kernel, [half, half], core, moved, t_table)
    keep, send = call(kick_kernel, [half, half], core, keep, swap(send), power, x_table, x_back)
    (rows,) = call(time_back_kernel, [(2 * NY, 128)], core, keep, swap(send), t_table)
    (out,) = call(last_kernel, [(2, NY, 128)], to_chips(rows), y_back)
    return out.reshape(2, 1, NY, 128)


def solution(mesh):
    torus = Mesh(mesh.devices.reshape(8, 4, 2, 2, mesh.shape["tm"]), ("z", "x", "h", "c", "t"))
    along_x = propagator(NX, -DIFFRACT)
    order = np.concatenate([np.arange(0, NX, 2), np.arange(1, NX, 2)])
    along_y_matrix = propagator(NY, -DIFFRACT)
    time_matrix = propagator(NT, DISPERSE).T
    tables = (
        stacked_rows(along_y_matrix),
        stacked_rows(along_y_matrix * well_phase(NY)[None, :]),
        np.stack([split(time_matrix.real), split(time_matrix.imag)]),
        real_block(along_x[order][:, order]),
        real_block((along_x * well_phase(NX)[None, :])[order][:, order]),
    )
    placed = P(None, SLAB, None, "t")
    inner = jax.shard_map(
        lambda field: on_device(field, *[jnp.asarray(table) for table in tables]),
        mesh=torus,
        in_specs=(placed,),
        out_specs=placed,
        check_vma=False,
    )
    return inner
```

profile of v0, /device:TPU:1, one launch (start us, length us, event | category | flops | bytes accessed | tf_op | source)
XLA Modules:
  0.0 109.8 jit_solution(7907816536007385422)
XLA Ops:
  0.0 2.2 %first_kernel.1 = (f32[512,128]{1,0:T(8,128)}, f32[32,128]{1,0:T(8,128)}) custom-call(f32[2,256,128]{2,1,0:T(8,128)} %bitcast.16, bf16[2,512,256]{2,1,0:T(8,128)(2,1)} %constant.18.clone.table_ref), custom_call_target="tpu_custom_call" | custom-call | tf_op jit(solution)/shard_map/first_kernel/pallas_call | solution.py:161
  2.2 0.0 copy-start.3
  2.2 23.3 %all-to-all-start = ((f32[256,2,128]{2,1,0:T(2,128)}), f32[256,2,128]{2,1,0:T(2,128)S(1)}, u32[]{:S(2)}, u32[]{:S(2)}) async-start(f32[256,2,128]{2,1,0:T(2,128)} %bitcast.17), calls=%async_computation | async-start | bytes 524288 | tf_op jit(solution)/shard_map/all_to_all | solution.py:171
  25.6 13.9 %all-to-all-done = f32[256,2,128]{2,1,0:T(2,128)S(1)} async-done(((f32[256,2,128]{2,1,0:T(2,128)}), f32[256,2,128]{2,1,0:T(2,128)S(1)}, u32[]{:S(2)}, u32[]{:S(2)}) %all-to-all-start) | async-done | bytes 262176 | tf_op jit(solution)/shard_map/all_to_all | solution.py:171
  39.5 0.0 copy-start
  39.5 0.7 copy-done
  40.2 3.0 %time_kernel.1 = (f32[2,64,256]{2,1,0:T(8,128)}, f32[2,64,256]{2,1,0:T(8,128)}) custom-call(s32[1]{0:T(128)} %bitcast.core_ref, f32[512,128]{1,0:T(8,128)} %bitcast.13, bf16[2,2,512,512]{3,2,1,0:T(8,128)(2,1)} %constant.20.clone.table_ref), custom_call_target="tpu_custom_call" | custom-call | tf_op jit(solution)/shard_map/time_kernel/pallas_call | solution.py:161
  43.2 4.5 %collective-permute-start = (f32[2,64,256]{2,1,0:T(8,128)}, f32[2,64,256]{2,1,0:T(8,128)S(1)}, u32[]{:S(2)}, u32[]{:S(2)}) collective-permute-start(f32[2,64,256]{2,1,0:T(8,128)} %get-tuple-element.13), channel_id=1, source_target_pairs={{0,4},{4,0},{1,5},{5,1},{2,6},{6,2},{3,7},{7,3},{8,12},{12,8},{9,1... | collective-permute-start | bytes 393224 | tf_op jit(solution)/shard_map/ppermute | solution.py:176
  47.6 0.0 copy-done.3
  47.6 12.4 %all_to_all.27 = f32[32,1,128]{2,1,0:T(1,128)S(1)} all-to-all(f32[32,1,128]{2,1,0:T(1,128)S(1)} %bitcast.19), channel_id=1, replica_groups=mesh['z'=8,'x'=4,'h'=2,'c'=2,'t'=4] {'z','x'}, dimensions={0} | all-to-all | bytes 32768 | tf_op jit(solution)/shard_map/all_to_all | solution.py:183
  60.0 0.1 reduce_sum.9
  60.1 11.5 %all_to_all.28 = f32[16,1,128]{2,1,0:T(1,128)} all-to-all(f32[16,1,128]{2,1,0:T(1,128)S(1)} %broadcast_in_dim.2), channel_id=1, replica_groups=mesh['z'=8,'x'=4,'h'=2,'c'=2,'t'=4] {'h','c','t'}, dimensions={0} | all-to-all | bytes 16384 | tf_op jit(solution)/shard_map/all_to_all | solution.py:185
  71.6 0.0 collective-permute-done.got_ref
  71.6 0.0 copy-start.2
  71.6 0.7 copy-done.2
  72.2 3.1 %kick_kernel.1 = (f32[2,64,256]{2,1,0:T(8,128)}, f32[2,64,256]{2,1,0:T(8,128)}) custom-call(s32[1]{0:T(128)} %bitcast.core_ref, f32[2,64,256]{2,1,0:T(8,128)} %get-tuple-element.12.keep_in_ref, f32[2,64,256]{2,1,0:T(8,128)} %copy-done.2, f32[16,128]{1,0:T(8,128)} %bitcast.18, bf16[2,256,256]{2,1,0:T(8,128)(2,1)} %constant.21.clone.table_ref, ...), custom_call_target="tpu_custom_call" | custom-call | tf_op jit(solution)/shard_map/kick_kernel/pallas_call | solution.py:161
  75.3 2.4 %collective-permute-start.1 = (f32[2,64,256]{2,1,0:T(8,128)}, f32[2,64,256]{2,1,0:T(8,128)S(1)}, u32[]{:S(2)}, u32[]{:S(2)}) collective-permute-start(f32[2,64,256]{2,1,0:T(8,128)} %get-tuple-element.16), channel_id=1, source_target_pairs={{0,4},{4,0},{1,5},{5,1},{2,6},{6,2},{3,7},{7,3},{8,12},{12,8},{9,1... | collective-permute-start | bytes 393224 | tf_op jit(solution)/shard_map/ppermute | solution.py:176
  77.8 1.2 %collective-permute-done.1.got_ref = f32[2,64,256]{2,1,0:T(8,128)S(1)} collective-permute-done((f32[2,64,256]{2,1,0:T(8,128)}, f32[2,64,256]{2,1,0:T(8,128)S(1)}, u32[]{:S(2)}, u32[]{:S(2)}) %collective-permute-start.1) | collective-permute-done | bytes 131104 | tf_op jit(solution)/shard_map/ppermute | solution.py:176
  78.9 0.0 copy-start.1
  78.9 0.6 copy-done.1
  79.6 3.0 %time_back_kernel.1 = f32[512,128]{1,0:T(8,128)} custom-call(s32[1]{0:T(128)} %bitcast.core_ref, f32[2,64,256]{2,1,0:T(8,128)} %get-tuple-element.15.keep_in_ref, f32[2,64,256]{2,1,0:T(8,128)} %copy-done.1, bf16[2,2,512,512]{3,2,1,0:T(8,128)(2,1)} %constant.20.clone.table_ref), custom_call_target="tpu_custom_call" | custom-call | tf_op jit(solution)/shard_map/time_back_kernel/pallas_call | solution.py:161
  82.6 25.0 %all_to_all.29 = f32[256,2,128]{2,1,0:T(2,128)} all-to-all(f32[256,2,128]{2,1,0:T(2,128)} %bitcast.15), channel_id=1, replica_groups=mesh['z'=8,'x'=4,'h'=2,'c'=2,'t'=4] {'z','x','h','t'}, dimensions={0} | all-to-all | bytes 524288 | tf_op jit(solution)/shard_map/all_to_all | solution.py:171
  107.6 2.2 %last_kernel.1 = f32[2,256,128]{2,1,0:T(8,128)} custom-call(f32[512,128]{1,0:T(8,128)} %bitcast.14, bf16[2,512,256]{2,1,0:T(8,128)(2,1)} %constant.19.clone.table_ref), custom_call_target="tpu_custom_call" | custom-call | tf_op jit(solution)/shard_map/last_kernel/pallas_call | solution.py:161
  (1 shorter events, 0.0 us)
Async XLA Ops:
  2.2 45.4 %copy-start.3 = (f32[32,128]{1,0:T(8,128)S(1)}, f32[32,128]{1,0:T(8,128)}, u32[]{:S(2)}) copy-start(f32[32,128]{1,0:T(8,128)} %get-tuple-element.14) | copy-start | bytes 49156
  2.2 37.3 %all-to-all-start = ((f32[256,2,128]{2,1,0:T(2,128)}), f32[256,2,128]{2,1,0:T(2,128)S(1)}, u32[]{:S(2)}, u32[]{:S(2)}) async-start(f32[256,2,128]{2,1,0:T(2,128)} %bitcast.17), calls=%async_computation | async-start | bytes 524288 | tf_op jit(solution)/shard_map/all_to_all | solution.py:171
  39.5 0.7 copy-start
  43.2 28.4 %collective-permute-start = (f32[2,64,256]{2,1,0:T(8,128)}, f32[2,64,256]{2,1,0:T(8,128)S(1)}, u32[]{:S(2)}, u32[]{:S(2)}) collective-permute-start(f32[2,64,256]{2,1,0:T(8,128)} %get-tuple-element.13), channel_id=1, source_target_pairs={{0,4},{4,0},{1,5},{5,1},{2,6},{6,2},{3,7},{7,3},{8,12},{12,8},{9,1... | collective-permute-start | bytes 393224 | tf_op jit(solution)/shard_map/ppermute | solution.py:176
  71.6 0.7 copy-start.2
  75.3 3.6 %collective-permute-start.1 = (f32[2,64,256]{2,1,0:T(8,128)}, f32[2,64,256]{2,1,0:T(8,128)S(1)}, u32[]{:S(2)}, u32[]{:S(2)}) collective-permute-start(f32[2,64,256]{2,1,0:T(8,128)} %get-tuple-element.16), channel_id=1, source_target_pairs={{0,4},{4,0},{1,5},{5,1},{2,6},{6,2},{3,7},{7,3},{8,12},{12,8},{9,1... | collective-permute-start | bytes 393224 | tf_op jit(solution)/shard_map/ppermute | solution.py:176
  78.9 0.6 copy-start.1
where the time goes:
time: 110 us
  blocking collectives  48.9 us (44%)
  starting transfers between devices  30.2 us (27%)
  waiting for transfers between devices  15.1 us (14%)
  Pallas kernels  13.5 us (12%)
  local copies, waits for them, and re-layouts  2.02 us (2%)
    all_to_all x1, blocking collectives, to_chips(): lax.all_to_all(rows.reshape(NY, 2, 128), CHIPS, split_axis=0, concat_axis...  25 us
    all_to_all x1, starting transfers between devices, to_chips(): lax.all_to_all(rows.reshape(NY, 2, 128), CHIPS, split_axis=0, concat_axis...  23.3 us
    all_to_all x1, waiting for transfers between devices, to_chips(): lax.all_to_all(rows.reshape(NY, 2, 128), CHIPS, split_axis=0, concat_axis...  13.9 us
    pallas_call x5, Pallas kernels, call(): pl.pallas_call(kernel, in_specs=specs, out_specs=[pl.BlockSpec(memory_spa...  13.5 us
    all_to_all x1, blocking collectives, on_device(): lax.all_to_all(power, ('z', 'x'), split_axis=0, concat_axis=0, tiled=True)  12.4 us
    all_to_all x1, blocking collectives, on_device(): lax.all_to_all(power, ('h', 'c', 't'), split_axis=0, concat_axis=0, tiled...  11.5 us
    ppermute x2, starting transfers between devices, swap(): return lax.ppermute(value, 'c', [(0, 1), (1, 0)])  6.88 us
  transfers between devices with their start and end apart: 3, of which 2 were waited for; matrix products, arithmetic and copies ran while one was open for 0% of the time, Pallas kernels for 0%

commit v1 on v0

v1 whole, which is shorter than its diff:
```python
import math

import jax
import jax.numpy as jnp
import ml_dtypes
import numpy as np
from jax import lax
from jax.experimental import pallas as pl
from jax.experimental.pallas import tpu as pltpu
from jax.sharding import Mesh
from jax.sharding import PartitionSpec as P

NX = 128
NY = 256
NT = 512
HALF_X = NX // 2
SLAB = ("z", "x", "h", "c")
CHIPS = ("z", "x", "h", "t")

TWO_PI = 2.0 * math.pi
DIFFRACT = 4.0
DISPERSE = 3.0
KERR = 0.05
WELL = 1.5
EPSILON = 1e-06


def propagator(length, weight):
    positions = np.arange(length)
    signed = np.where(2 * positions < length, positions, positions - length)
    angle = weight * (signed * (TWO_PI / length)) ** 2
    kernel = np.fft.ifft(np.exp(1j * angle))
    return kernel[(positions[:, None] - positions[None, :]) % length]


def split(matrix):
    full = matrix.astype(np.float32)
    high = full.astype(ml_dtypes.bfloat16)
    low = (matrix - high.astype(np.float64)).astype(ml_dtypes.bfloat16)
    return np.stack([high, low])


def stacked_rows(matrix):
    return split(np.concatenate([matrix.real, matrix.imag], axis=0))


def real_block(matrix):
    return split(np.block([[matrix.real, -matrix.imag], [matrix.imag, matrix.real]]))


def pieces(value):
    high = value.astype(jnp.bfloat16)
    return high, (value - high.astype(jnp.float32)).astype(jnp.bfloat16)


def dot(left, right):
    return jnp.dot(left, right, preferred_element_type=jnp.float32)


def along_y(real, imag, table_ref):
    high, low = pieces(jnp.concatenate([real, imag], axis=1))
    r = dot(table_ref[0], high) + (dot(table_ref[0], low) + dot(table_ref[1], high))
    return r[:NY, :128] - r[NY:, 128:], r[:NY, 128:] + r[NY:, :128]


def along_t(real, imag, table_ref):
    rows = real.shape[0]
    high, low = pieces(jnp.concatenate([real, imag], axis=0))
    both = jnp.concatenate([high, low], axis=0)

    def product(k):
        p = dot(both, table_ref[k, 0])
        return p[: 2 * rows] + (p[2 * rows :] + dot(high, table_ref[k, 1]))

    by_real = product(0)
    by_imag = product(1)
    return by_real[:rows] - by_imag[rows:], by_real[rows:] + by_imag[:rows]


def turns(angle):
    count = jnp.floor(angle * (2.0 / math.pi) + 0.5)
    rest = ((angle - count * 1.5703125) - count * 4.837512969970703125e-4) - count * 7.54978995489188216e-8
    quadrant = count.astype(jnp.int32)
    square = rest * rest
    sine = rest + rest * square * (-1.6666654611e-1 + square * (8.3321608736e-3 - 1.9515295891e-4 * square))
    cosine = (1.0 - 0.5 * square) + square * square * (
        4.166664568298827e-2 + square * (-1.388731625493765e-3 + 2.443315711809948e-5 * square)
    )
    odd = (quadrant & 1) == 1
    cos_turn = jnp.where(odd, sine, cosine)
    sin_turn = jnp.where(odd, cosine, sine)
    return (
        jnp.where(((quadrant + 1) & 2) == 2, -cos_turn, cos_turn),
        jnp.where((quadrant & 2) == 2, -sin_turn, sin_turn),
    )


def first_kernel(field_ref, table_ref, out_ref):
    real = field_ref[0]
    imag = field_ref[1]
    out_real, out_imag = along_y(real, imag, table_ref)
    out_ref[pl.ds(0, NY, stride=3), :] = out_real
    out_ref[pl.ds(1, NY, stride=3), :] = out_imag
    power = jnp.sum(real * real + imag * imag, axis=0, keepdims=True)
    out_ref[pl.ds(2, NY, stride=3), :] = jnp.broadcast_to(power, (NY, 128))


def time_kernel(in_ref, table_ref, out_ref):
    def part(p):
        return jnp.concatenate([in_ref[pl.ds(3 * g + p, HALF_X, stride=12), :] for g in range(4)], axis=1)

    outs = along_t(part(0), part(1), table_ref)
    out_ref[:HALF_X] = outs[0]
    out_ref[HALF_X:NX] = outs[1]
    power = jnp.sum(in_ref[pl.ds(2, NY, stride=3), :], axis=0, keepdims=True)
    out_ref[NX:, :128] = jnp.broadcast_to(power, (8, 128))


def kick_kernel(place_ref, mine_ref, other_ref, x_table_ref, t_table_ref, out_ref, work_ref):
    core = place_ref[0]
    lower = core == 0
    total = jnp.sum(mine_ref[NX : NX + 1, :128] + other_ref[NX : NX + 1, :128], axis=1, keepdims=True)
    scale = 1.0 / jnp.sqrt(total * (1.0 / (NX * NY * NT)) + EPSILON)
    for p in range(2):
        kept = mine_ref[p * HALF_X : (p + 1) * HALF_X]
        got = other_ref[p * HALF_X : (p + 1) * HALF_X]
        work_ref[p * NX : p * NX + HALF_X] = jnp.where(lower, kept, got)
        work_ref[p * NX + HALF_X : (p + 1) * NX] = jnp.where(lower, got, kept)
    high, low = pieces(work_ref[...])
    for parity in range(2):
        table = x_table_ref[0, parity]
        first = dot(table, high) + (dot(table, low) + dot(x_table_ref[1, parity], high))
        for p in range(2):
            work_ref[p * NX + parity * HALF_X : p * NX + (parity + 1) * HALF_X] = first[p * HALF_X : (p + 1) * HALF_X]
    place_y = (place_ref[1].astype(jnp.float32) - (NY - 1) / 2.0) / (NY / 2.0)
    row = lax.broadcasted_iota(jnp.int32, (8, NT), 0)
    for start in range(0, NX, 8):
        parity, base = divmod(start, HALF_X)
        place_x = ((2 * (base + row) + parity).astype(jnp.float32) - (NX - 1) / 2.0) / (NX / 2.0)
        real = work_ref[start : start + 8] * scale
        imag = work_ref[NX + start : NX + start + 8] * scale
        cos_turn, sin_turn = turns(KERR * (real * real + imag * imag) - WELL * (place_x * place_x + place_y * place_y))
        work_ref[start : start + 8] = real * cos_turn - imag * sin_turn
        work_ref[NX + start : NX + start + 8] = real * sin_turn + imag * cos_turn
    high, low = pieces(work_ref[...])
    table = x_table_ref[0, core]
    second = dot(table, high) + (dot(table, low) + dot(x_table_ref[1, core], high))
    outs = along_t(second[:HALF_X], second[HALF_X:], t_table_ref)
    for p in range(2):
        for g in range(4):
            out_ref[pl.ds(2 * g + p, HALF_X, stride=8), :] = outs[p][:, 128 * g : 128 * (g + 1)]


def last_kernel(in_ref, table_ref, out_ref):
    real = in_ref[pl.ds(0, NY, stride=2), :]
    imag = in_ref[pl.ds(1, NY, stride=2), :]
    out_real, out_imag = along_y(real, imag, table_ref)
    out_ref[0] = out_real
    out_ref[1] = out_imag


def call(kernel, shape, *args, scratch=()):
    return pl.pallas_call(
        kernel,
        in_specs=[pl.BlockSpec(memory_space=pltpu.SMEM if a.dtype == jnp.int32 else pltpu.VMEM) for a in args],
        out_specs=pl.BlockSpec(memory_space=pltpu.VMEM),
        out_shape=jax.ShapeDtypeStruct(shape, jnp.float32),
        scratch_shapes=[pltpu.VMEM(s, jnp.float32) for s in scratch],
        compiler_params=pltpu.CompilerParams(vmem_limit_bytes=16 * 2**20),
        name=kernel.__name__,
    )(*args)


def to_chips(rows, count):
    moved = lax.all_to_all(rows.reshape(NY, 1, count * 128), CHIPS, split_axis=0, concat_axis=0, tiled=True)
    return moved.reshape(count * NY, 128)


def on_device(field, y_table, t_table, x_table):
    place = jnp.stack([lax.axis_index("c"), lax.axis_index(CHIPS)]).astype(jnp.int32)
    rows = to_chips(call(first_kernel, (3 * NY, 128), field.reshape(2, NY, 128), y_table), 3)
    mine = call(time_kernel, (NX + 8, NT), rows, t_table)
    other = lax.ppermute(mine, "c", [(0, 1), (1, 0)])
    rows = call(kick_kernel, (2 * NY, 128), place, mine, other, x_table, t_table, scratch=[(2 * NX, NT)])
    out = call(last_kernel, (2, NY, 128), to_chips(rows, 2), y_table)
    return out.reshape(2, 1, NY, 128)


def solution(mesh):
    torus = Mesh(mesh.devices.reshape(8, 4, 2, 2, mesh.shape["tm"]), ("z", "x", "h", "c", "t"))
    along_x = propagator(NX, -DIFFRACT)
    order = np.concatenate([np.arange(0, NX, 2), np.arange(1, NX, 2)])
    along_y_matrix = propagator(NY, -DIFFRACT)
    time_matrix = propagator(NT, DISPERSE).T
    x_block = real_block(along_x[order][:, order])
    x_block = x_block.reshape(2, 2, 2, HALF_X, 2 * NX).transpose(0, 2, 1, 3, 4).reshape(2, 2, NX, 2 * NX)
    tables = (
        stacked_rows(along_y_matrix),
        np.stack([split(time_matrix.real), split(time_matrix.imag)]),
        x_block,
    )
    placed = P(None, SLAB, None, "t")
    inner = jax.shard_map(
        lambda field: on_device(field, *[jnp.asarray(table) for table in tables]),
        mesh=torus,
        in_specs=(placed,),
        out_specs=placed,
        check_vma=False,
    )
    return inner
```

time: 110 us -> 77.1 us (0.70)
  starting transfers between devices: 30.2 us -> 4.74 us
  blocking collectives: 48.9 us -> 63.1 us
  waiting for transfers between devices: 15.1 us -> 1.08 us
  Pallas kernels: 13.5 us -> 4.14 us
  local copies, waits for them, and re-layouts: 2.02 us -> 3.6 us
    all_to_all x1 -> x0, starting transfers between devices: 23.3 us -> none  [to_chips(): lax.all_to_all(rows.reshape(NY, 2, 128), CHIPS, split_axis=0, concat_axis...]
    all_to_all x3 -> x2, blocking collectives: 48.9 us -> 63.1 us  [to_chips(): lax.all_to_all(rows.reshape(NY, 1, count * 128), CHIPS, split_axis=0, con...]
    all_to_all x1 -> x0, waiting for transfers between devices: 13.9 us -> none  [to_chips(): lax.all_to_all(rows.reshape(NY, 2, 128), CHIPS, split_axis=0, concat_axis...]
    pallas_call x5 -> x4, Pallas kernels: 13.5 us -> 4.14 us  [call(): pl.pallas_call(kernel, in_specs=[pl.BlockSpec(memory_space=pltpu.SMEM if...]
    ppermute x2 -> x1, starting transfers between devices: 6.88 us -> 4.74 us  [on_device(): other = lax.ppermute(mine, 'c', [(0, 1), (1, 0)])]
    unnamed x8 -> x12, local copies, waits for them, and re-layouts: 2.01 us -> 3.6 us
  transfers between devices with their start and end apart: 3 -> 1, of which waited for: 2 -> 1; matrix products, arithmetic and copies ran while one was open for 0% -> 0% of each run, Pallas kernels for 0% -> 0%
where the time goes in v1:
time: 77.1 us; the launch traced here: 76.8 us
  blocking collectives  63.1 us (82%)
  starting transfers between devices  4.74 us (6%)
  Pallas kernels  4.14 us (5%)
  local copies, waits for them, and re-layouts  3.6 us (5%)
  waiting for transfers between devices  1.08 us (1%)
    all_to_all x2, blocking collectives, to_chips(): lax.all_to_all(rows.reshape(NY, 1, count * 128), CHIPS, split_axis=0, con...  63.1 us
    ppermute x1, starting transfers between devices, on_device(): other = lax.ppermute(mine, 'c', [(0, 1), (1, 0)])  4.74 us
    pallas_call x4, Pallas kernels, call(): pl.pallas_call(kernel, in_specs=[pl.BlockSpec(memory_space=pltpu.SMEM if...  4.14 us
    unnamed x12, local copies, waits for them, and re-layouts  3.6 us
  transfers between devices with their start and end apart: 1, of which 1 were waited for; matrix products, arithmetic and copies ran while one was open for 0% of the time, Pallas kernels for 0%

profile of v1, /device:TPU:1, one launch (start us, length us, event | category | flops | bytes accessed | tf_op | source)
XLA Modules:
  0.0 76.8 jit_solution(11299973107909706368)
XLA Ops:
  0.0 0.0 copy-start.2
  0.0 1.0 %copy-done.2 = bf16[2,512,256]{2,1,0:T(8,128)(2,1)S(1)} copy-done((bf16[2,512,256]{2,1,0:T(8,128)(2,1)S(1)}, bf16[2,512,256]{2,1,0:T(8,128)(2,1)}, u32[]{:S(2)}) %copy-start.2) | copy-done | bytes 524312
  1.0 0.0 copy-start.4
  1.0 0.9 %copy-done.4 = f32[2,1,256,128]{3,2,1,0:T(8,128)S(1)} copy-done((f32[2,1,256,128]{3,2,1,0:T(8,128)S(1)}, f32[2,1,256,128]{3,2,1,0:T(8,128)}, u32[]{:S(2)}) %copy-start.4) | copy-done | bytes 262168
  2.0 0.4 first_kernel.1
  2.4 0.0 copy-start.5
  2.4 39.7 %all_to_all.10 = f32[256,1,384]{2,1,0:T(1,128)S(1)} all-to-all(f32[256,1,384]{2,1,0:T(1,128)S(1)} %bitcast.10), channel_id=1, replica_groups=mesh['z'=8,'x'=4,'h'=2,'c'=2,'t'=4] {'z','x','h','t'}, dimensions={0} | all-to-all | bytes 786432 | tf_op jit(solution)/shard_map/all_to_all | solution.py:175
  42.1 0.0 copy-start
  42.1 1.6 %copy-done = bf16[2,2,512,512]{3,2,1,0:T(8,128)(2,1)S(1)} copy-done((bf16[2,2,512,512]{3,2,1,0:T(8,128)(2,1)S(1)}, bf16[2,2,512,512]{3,2,1,0:T(8,128)(2,1)}, u32[]{:S(2)}) %copy-start) | copy-done | bytes 2097176
  43.7 0.0 copy-start.1
  43.7 0.6 time_kernel.1.mine_ref
  44.2 0.0 copy-start.3
  44.3 4.7 %collective-permute-start = (f32[136,512]{1,0:T(8,128)S(1)}, f32[136,512]{1,0:T(8,128)S(1)}, u32[]{:S(2)}, u32[]{:S(2)}) collective-permute-start(f32[136,512]{1,0:T(8,128)S(1)} %time_kernel.1.mine_ref), channel_id=1, source_target_pairs={{0,4},{4,0},{1,5},{5,1},{2,6},{6,2},{3,7},{7,3},{8,12},{12,8},{9,1... | collective-permute-start | bytes 835592 | tf_op jit(solution)/shard_map/ppermute | solution.py:183
  49.0 0.1 pad_add_fusion.place_ref
  49.1 1.1 %collective-permute-done.other_ref = f32[136,512]{1,0:T(8,128)S(1)} collective-permute-done((f32[136,512]{1,0:T(8,128)S(1)}, f32[136,512]{1,0:T(8,128)S(1)}, u32[]{:S(2)}, u32[]{:S(2)}) %collective-permute-start) | collective-permute-done | bytes 278560 | tf_op jit(solution)/shard_map/ppermute | solution.py:183
  50.2 0.0 copy-done.5
  50.2 0.0 copy-done.1
  50.2 2.1 %kick_kernel.1 = f32[512,128]{1,0:T(8,128)S(1)} custom-call(s32[2]{0:T(128)S(1)} %pad_add_fusion.place_ref, f32[136,512]{1,0:T(8,128)S(1)} %time_kernel.1.mine_ref, f32[136,512]{1,0:T(8,128)S(1)} %collective-permute-done.other_ref, bf16[2,2,128,256]{3,2,1,0:T(8,128)(2,1)S(1)} %copy-done.5, bf16[2,2,512,512]{3,2,1,0:T(8,128)(2,1)S(1)} %copy-done.1), custom_call_target="tpu_custom_call" | custom-call | tf_op jit(solution)/shard_map/kick_kernel/pallas_call | solution.py:163
  52.3 23.4 %all_to_all.11 = f32[256,1,256]{2,1,0:T(1,128)S(1)} all-to-all(f32[256,1,256]{2,1,0:T(1,128)S(1)} %bitcast.13), channel_id=1, replica_groups=mesh['z'=8,'x'=4,'h'=2,'c'=2,'t'=4] {'z','x','h','t'}, dimensions={0} | all-to-all | bytes 524288 | tf_op jit(solution)/shard_map/all_to_all | solution.py:175
  75.7 0.0 copy-done.3
  75.7 1.1 %last_kernel.1 = f32[2,256,128]{2,1,0:T(8,128)} custom-call(f32[512,128]{1,0:T(8,128)S(1)} %bitcast.12, bf16[2,512,256]{2,1,0:T(8,128)(2,1)S(1)} %copy-done.3), custom_call_target="tpu_custom_call" | custom-call | tf_op jit(solution)/shard_map/last_kernel/pallas_call | solution.py:163
Async XLA Ops:
  0.0 1.0 %copy-start.2 = (bf16[2,512,256]{2,1,0:T(8,128)(2,1)S(1)}, bf16[2,512,256]{2,1,0:T(8,128)(2,1)}, u32[]{:S(2)}) copy-start(bf16[2,512,256]{2,1,0:T(8,128)(2,1)} %constant.33.clone.table_ref) | copy-start | bytes 1572868
  1.0 0.9 %copy-start.4 = (f32[2,1,256,128]{3,2,1,0:T(8,128)S(1)}, f32[2,1,256,128]{3,2,1,0:T(8,128)}, u32[]{:S(2)}) copy-start(f32[2,1,256,128]{3,2,1,0:T(8,128)} %param.4) | copy-start | bytes 786436
  2.4 47.8 %copy-start.5 = (bf16[2,2,128,256]{3,2,1,0:T(8,128)(2,1)S(1)}, bf16[2,2,128,256]{3,2,1,0:T(8,128)(2,1)}, u32[]{:S(2)}) copy-start(bf16[2,2,128,256]{3,2,1,0:T(8,128)(2,1)} %constant.35.clone.x_table_ref) | copy-start | bytes 786436
  42.1 1.6 %copy-start = (bf16[2,2,512,512]{3,2,1,0:T(8,128)(2,1)S(1)}, bf16[2,2,512,512]{3,2,1,0:T(8,128)(2,1)}, u32[]{:S(2)}) copy-start(bf16[2,2,512,512]{3,2,1,0:T(8,128)(2,1)} %constant.34.clone.table_ref.t_table_ref) | copy-start | bytes 6291460
  43.7 6.5 %copy-start.1 = (bf16[2,2,512,512]{3,2,1,0:T(8,128)(2,1)S(1)}, bf16[2,2,512,512]{3,2,1,0:T(8,128)(2,1)}, u32[]{:S(2)}) copy-start(bf16[2,2,512,512]{3,2,1,0:T(8,128)(2,1)} %constant.34.clone.table_ref.t_table_ref) | copy-start | bytes 6291460
  44.2 31.5 %copy-start.3 = (bf16[2,512,256]{2,1,0:T(8,128)(2,1)S(1)}, bf16[2,512,256]{2,1,0:T(8,128)(2,1)}, u32[]{:S(2)}) copy-start(bf16[2,512,256]{2,1,0:T(8,128)(2,1)} %constant.33.clone.table_ref) | copy-start | bytes 1572868
  44.3 5.9 %collective-permute-start = (f32[136,512]{1,0:T(8,128)S(1)}, f32[136,512]{1,0:T(8,128)S(1)}, u32[]{:S(2)}, u32[]{:S(2)}) collective-permute-start(f32[136,512]{1,0:T(8,128)S(1)} %time_kernel.1.mine_ref), channel_id=1, source_target_pairs={{0,4},{4,0},{1,5},{5,1},{2,6},{6,2},{3,7},{7,3},{8,12},{12,8},{9,1... | collective-permute-start | bytes 835592 | tf_op jit(solution)/shard_map/ppermute | solution.py:183

commit v2 on v1

--- a/solution.py
+++ b/solution.py
@@ -16,6 +16,9 @@
 HALF_X = NX // 2
 SLAB = ("z", "x", "h", "c")
 CHIPS = ("z", "x", "h", "t")
+DEVICES = ("z", "x", "h", "c", "t")
+FLIP_X = 37
+FLIP = FLIP_X * 4
 
 TWO_PI = 2.0 * math.pi
 DIFFRACT = 4.0
@@ -136,7 +139,7 @@
     row = lax.broadcasted_iota(jnp.int32, (8, NT), 0)
     for start in range(0, NX, 8):
         parity, base = divmod(start, HALF_X)
-        place_x = ((2 * (base + row) + parity).astype(jnp.float32) - (NX - 1) / 2.0) / (NX / 2.0)
+        place_x = ((2 * ((base + row) ^ FLIP_X) + parity).astype(jnp.float32) - (NX - 1) / 2.0) / (NX / 2.0)
         real = work_ref[start : start + 8] * scale
         imag = work_ref[NX + start : NX + start + 8] * scale
         cos_turn, sin_turn = turns(KERR * (real * real + imag * imag) - WELL * (place_x * place_x + place_y * place_y))
@@ -171,13 +174,28 @@
     )(*args)
 
 
+def groups():
+    found = []
+    for core in range(2):
+        chips = [position ^ FLIP for position in range(NY)]
+        found.append([(chip >> 2) * 8 + core * 4 + (chip & 3) for chip in chips])
+    return found
+
+
 def to_chips(rows, count):
-    moved = lax.all_to_all(rows.reshape(NY, 1, count * 128), CHIPS, split_axis=0, concat_axis=0, tiled=True)
+    moved = lax.all_to_all(
+        rows.reshape(NY, 1, count * 128),
+        DEVICES,
+        split_axis=0,
+        concat_axis=0,
+        tiled=True,
+        axis_index_groups=groups(),
+    )
     return moved.reshape(count * NY, 128)
 
 
 def on_device(field, y_table, t_table, x_table):
-    place = jnp.stack([lax.axis_index("c"), lax.axis_index(CHIPS)]).astype(jnp.int32)
+    place = jnp.stack([lax.axis_index("c"), lax.axis_index(CHIPS) ^ FLIP]).astype(jnp.int32)
     rows = to_chips(call(first_kernel, (3 * NY, 128), field.reshape(2, NY, 128), y_table), 3)
     mine = call(time_kernel, (NX + 8, NT), rows, t_table)
     other = lax.ppermute(mine, "c", [(0, 1), (1, 0)])
@@ -189,7 +207,8 @@
 def solution(mesh):
     torus = Mesh(mesh.devices.reshape(8, 4, 2, 2, mesh.shape["tm"]), ("z", "x", "h", "c", "t"))
     along_x = propagator(NX, -DIFFRACT)
-    order = np.concatenate([np.arange(0, NX, 2), np.arange(1, NX, 2)])
+    even = 2 * (np.arange(HALF_X) ^ FLIP_X)
+    order = np.concatenate([even, even + 1])
     along_y_matrix = propagator(NY, -DIFFRACT)
     time_matrix = propagator(NT, DISPERSE).T
     x_block = real_block(along_x[order][:, order])

time: 77.1 us -> 71.3 us (0.925)
  blocking collectives: 63.1 us -> 58.7 us
  starting transfers between devices: 4.74 us -> 3.27 us
    all_to_all x2, blocking collectives: 63.1 us -> 58.7 us  [to_chips(): lax.all_to_all(rows.reshape(NY, 1, count * 128), DEVICES, split_axis=0, c...]
    ppermute x1, starting transfers between devices: 4.74 us -> 3.27 us  [on_device(): other = lax.ppermute(mine, 'c', [(0, 1), (1, 0)])]
where the time goes in v2:
time: 71.3 us; the launch traced here: 70.9 us
  blocking collectives  58.7 us (82%)
  Pallas kernels  4.13 us (6%)
  local copies, waits for them, and re-layouts  3.6 us (5%)
  starting transfers between devices  3.27 us (5%)
  waiting for transfers between devices  1.08 us (2%)
    all_to_all x2, blocking collectives, to_chips(): lax.all_to_all(rows.reshape(NY, 1, count * 128), DEVICES, split_axis=0, c...  58.7 us
    pallas_call x4, Pallas kernels, call(): pl.pallas_call(kernel, in_specs=[pl.BlockSpec(memory_space=pltpu.SMEM if...  4.13 us
    unnamed x12, local copies, waits for them, and re-layouts  3.6 us
    ppermute x1, starting transfers between devices, on_device(): other = lax.ppermute(mine, 'c', [(0, 1), (1, 0)])  3.27 us
  transfers between devices with their start and end apart: 1, of which 1 were waited for; matrix products, arithmetic and copies ran while one was open for 0% of the time, Pallas kernels for 0%

profile of v2, /device:TPU:1, one launch (start us, length us, event | category | flops | bytes accessed | tf_op | source)
XLA Modules:
  0.0 70.9 jit_solution(17681102132145178853)
XLA Ops:
  0.0 0.0 copy-start.2
  0.0 1.0 %copy-done.2 = bf16[2,512,256]{2,1,0:T(8,128)(2,1)S(1)} copy-done((bf16[2,512,256]{2,1,0:T(8,128)(2,1)S(1)}, bf16[2,512,256]{2,1,0:T(8,128)(2,1)}, u32[]{:S(2)}) %copy-start.2) | copy-done | bytes 524312
  1.0 0.0 copy-start.4
  1.0 0.9 %copy-done.4 = f32[2,1,256,128]{3,2,1,0:T(8,128)S(1)} copy-done((f32[2,1,256,128]{3,2,1,0:T(8,128)S(1)}, f32[2,1,256,128]{3,2,1,0:T(8,128)}, u32[]{:S(2)}) %copy-start.4) | copy-done | bytes 262168
  2.0 0.4 first_kernel.1
  2.4 0.0 copy-start.5
  2.4 34.3 %all_to_all.10 = f32[256,1,384]{2,1,0:T(1,128)S(1)} all-to-all(f32[256,1,384]{2,1,0:T(1,128)S(1)} %bitcast.10), channel_id=1, replica_groups={{296,297,298,299,288,289,290,291,312,313,314,315,304,305,306,307,264,26..., dimensions={0} | all-to-all | bytes 786432 | tf_op jit(solution)/shard_map/all_to_all | solution.py:186
  36.7 0.0 copy-start
  36.7 1.6 %copy-done = bf16[2,2,512,512]{3,2,1,0:T(8,128)(2,1)S(1)} copy-done((bf16[2,2,512,512]{3,2,1,0:T(8,128)(2,1)S(1)}, bf16[2,2,512,512]{3,2,1,0:T(8,128)(2,1)}, u32[]{:S(2)}) %copy-start) | copy-done | bytes 2097176
  38.3 0.0 copy-start.1
  38.3 0.6 time_kernel.1.mine_ref
  38.8 0.0 copy-start.3
  38.9 3.3 %collective-permute-start = (f32[136,512]{1,0:T(8,128)S(1)}, f32[136,512]{1,0:T(8,128)S(1)}, u32[]{:S(2)}, u32[]{:S(2)}) collective-permute-start(f32[136,512]{1,0:T(8,128)S(1)} %time_kernel.1.mine_ref), channel_id=1, source_target_pairs={{0,4},{4,0},{1,5},{5,1},{2,6},{6,2},{3,7},{7,3},{8,12},{12,8},{9,1... | collective-permute-start | bytes 835592 | tf_op jit(solution)/shard_map/ppermute | solution.py:201
  42.1 0.1 pad_add_fusion.place_ref
  42.2 1.1 %collective-permute-done.other_ref = f32[136,512]{1,0:T(8,128)S(1)} collective-permute-done((f32[136,512]{1,0:T(8,128)S(1)}, f32[136,512]{1,0:T(8,128)S(1)}, u32[]{:S(2)}, u32[]{:S(2)}) %collective-permute-start) | collective-permute-done | bytes 278560 | tf_op jit(solution)/shard_map/ppermute | solution.py:201
  43.3 0.0 copy-done.5
  43.3 0.0 copy-done.1
  43.3 2.1 %kick_kernel.1 = f32[512,128]{1,0:T(8,128)S(1)} custom-call(s32[2]{0:T(128)S(1)} %pad_add_fusion.place_ref, f32[136,512]{1,0:T(8,128)S(1)} %time_kernel.1.mine_ref, f32[136,512]{1,0:T(8,128)S(1)} %collective-permute-done.other_ref, bf16[2,2,128,256]{3,2,1,0:T(8,128)(2,1)S(1)} %copy-done.5, bf16[2,2,512,512]{3,2,1,0:T(8,128)(2,1)S(1)} %copy-done.1), custom_call_target="tpu_custom_call" | custom-call | tf_op jit(solution)/shard_map/kick_kernel/pallas_call | solution.py:166
  45.4 24.4 %all_to_all.11 = f32[256,1,256]{2,1,0:T(1,128)S(1)} all-to-all(f32[256,1,256]{2,1,0:T(1,128)S(1)} %bitcast.13), channel_id=1, replica_groups={{296,297,298,299,288,289,290,291,312,313,314,315,304,305,306,307,264,26..., dimensions={0} | all-to-all | bytes 524288 | tf_op jit(solution)/shard_map/all_to_all | solution.py:186
  69.9 0.0 copy-done.3
  69.9 1.1 %last_kernel.1 = f32[2,256,128]{2,1,0:T(8,128)} custom-call(f32[512,128]{1,0:T(8,128)S(1)} %bitcast.12, bf16[2,512,256]{2,1,0:T(8,128)(2,1)S(1)} %copy-done.3), custom_call_target="tpu_custom_call" | custom-call | tf_op jit(solution)/shard_map/last_kernel/pallas_call | solution.py:166
Async XLA Ops:
  0.0 1.0 %copy-start.2 = (bf16[2,512,256]{2,1,0:T(8,128)(2,1)S(1)}, bf16[2,512,256]{2,1,0:T(8,128)(2,1)}, u32[]{:S(2)}) copy-start(bf16[2,512,256]{2,1,0:T(8,128)(2,1)} %constant.35.clone.table_ref) | copy-start | bytes 1572868
  1.0 0.9 %copy-start.4 = (f32[2,1,256,128]{3,2,1,0:T(8,128)S(1)}, f32[2,1,256,128]{3,2,1,0:T(8,128)}, u32[]{:S(2)}) copy-start(f32[2,1,256,128]{3,2,1,0:T(8,128)} %param.4) | copy-start | bytes 786436
  2.4 40.9 %copy-start.5 = (bf16[2,2,128,256]{3,2,1,0:T(8,128)(2,1)S(1)}, bf16[2,2,128,256]{3,2,1,0:T(8,128)(2,1)}, u32[]{:S(2)}) copy-start(bf16[2,2,128,256]{3,2,1,0:T(8,128)(2,1)} %constant.37.clone.x_table_ref) | copy-start | bytes 786436
  36.7 1.6 %copy-start = (bf16[2,2,512,512]{3,2,1,0:T(8,128)(2,1)S(1)}, bf16[2,2,512,512]{3,2,1,0:T(8,128)(2,1)}, u32[]{:S(2)}) copy-start(bf16[2,2,512,512]{3,2,1,0:T(8,128)(2,1)} %constant.36.clone.table_ref.t_table_ref) | copy-start | bytes 6291460
  38.3 5.0 %copy-start.1 = (bf16[2,2,512,512]{3,2,1,0:T(8,128)(2,1)S(1)}, bf16[2,2,512,512]{3,2,1,0:T(8,128)(2,1)}, u32[]{:S(2)}) copy-start(bf16[2,2,512,512]{3,2,1,0:T(8,128)(2,1)} %constant.36.clone.table_ref.t_table_ref) | copy-start | bytes 6291460
  38.8 31.0 %copy-start.3 = (bf16[2,512,256]{2,1,0:T(8,128)(2,1)S(1)}, bf16[2,512,256]{2,1,0:T(8,128)(2,1)}, u32[]{:S(2)}) copy-start(bf16[2,512,256]{2,1,0:T(8,128)(2,1)} %constant.35.clone.table_ref) | copy-start | bytes 1572868
  38.9 4.4 %collective-permute-start = (f32[136,512]{1,0:T(8,128)S(1)}, f32[136,512]{1,0:T(8,128)S(1)}, u32[]{:S(2)}, u32[]{:S(2)}) collective-permute-start(f32[136,512]{1,0:T(8,128)S(1)} %time_kernel.1.mine_ref), channel_id=1, source_target_pairs={{0,4},{4,0},{1,5},{5,1},{2,6},{6,2},{3,7},{7,3},{8,12},{12,8},{9,1... | collective-permute-start | bytes 835592 | tf_op jit(solution)/shard_map/ppermute | solution.py:201

commit v3 on v2

v3 whole, which is shorter than its diff:
```python
import math

import jax
import jax.numpy as jnp
import ml_dtypes
import numpy as np
from jax import lax
from jax.experimental import pallas as pl
from jax.experimental.pallas import tpu as pltpu
from jax.sharding import Mesh
from jax.sharding import PartitionSpec as P

NX = 128
NY = 256
NT = 512
HALF_X = NX // 2
SLAB = ("z", "x", "h", "c")
CHIPS = ("z", "x", "h", "t")
DEVICES = ("z", "x", "h", "c", "t")
EXTENT = (8, 4, 8)
ROOT = (4, 2, 4)
HOP = (0.46, 0.41, 0.54)

TWO_PI = 2.0 * math.pi
DIFFRACT = 4.0
DISPERSE = 3.0
KERR = 0.05
WELL = 1.5
EPSILON = 1e-06


def propagator(length, weight):
    positions = np.arange(length)
    signed = np.where(2 * positions < length, positions, positions - length)
    angle = weight * (signed * (TWO_PI / length)) ** 2
    kernel = np.fft.ifft(np.exp(1j * angle))
    return kernel[(positions[:, None] - positions[None, :]) % length]


def split(matrix):
    full = matrix.astype(np.float32)
    high = full.astype(ml_dtypes.bfloat16)
    low = (matrix - high.astype(np.float64)).astype(ml_dtypes.bfloat16)
    return np.stack([high, low])


def run_order():
    def cost(run):
        place = (run >> 3, (run >> 1) & 3, 4 * (run & 1))
        away = [abs(p - r) for p, r in zip(place, ROOT)]
        return sum(w * min(d, n - d) for w, d, n in zip(HOP, away, EXTENT))

    root = ROOT[0] * 8 + ROOT[1] * 2 + ROOT[2] // 4
    return [root] + sorted((run for run in range(HALF_X) if run != root), key=lambda run: (-cost(run), run))


def real_block(matrix):
    return split(np.block([[matrix.real, -matrix.imag], [matrix.imag, matrix.real]]))


def pieces(value):
    high = value.astype(jnp.bfloat16)
    return high, (value - high.astype(jnp.float32)).astype(jnp.bfloat16)


def dot(left, right):
    return jnp.dot(left, right, preferred_element_type=jnp.float32)


def along_y(real, imag, table_ref):
    straight = jnp.concatenate([real, imag], axis=1)
    half = NY // 2
    data = jnp.concatenate([straight, jnp.concatenate([straight[half:], straight[:half]], axis=0)], axis=1)
    high, low = pieces(data)
    r = dot(table_ref[0], high) + (dot(table_ref[0], low) + dot(table_ref[1], high))
    by_real = r[:half]
    by_imag = r[half:]
    reals = [by_real[:, j : j + 128] - by_imag[:, j + 128 : j + 256] for j in (0, 256)]
    imags = [by_real[:, j + 128 : j + 256] + by_imag[:, j : j + 128] for j in (0, 256)]
    return reals, imags


def along_t(blocks, table_ref):
    rows = blocks[0][0].shape[0]
    split_blocks = [[pieces(block) for block in part] for part in blocks]

    def pairs(k):
        return jnp.concatenate(
            [
                jnp.concatenate([split_blocks[p][g][k], split_blocks[p][(g + 1) % 4][k]], axis=1)
                for g in range(4)
                for p in range(2)
            ],
            axis=0,
        )

    high, low = pairs(0), pairs(1)
    r = dot(high, table_ref[0]) + (dot(low, table_ref[0]) + dot(high, table_ref[1]))

    def product(g, p):
        upper = (2 * g + p) * rows
        lower = (2 * ((g + 2) % 4) + p) * rows
        return r[upper : upper + rows, :256] + r[lower : lower + rows, 256:]

    outs = [[], []]
    for g in range(4):
        from_real = product(g, 0)
        from_imag = product(g, 1)
        outs[0].append(from_real[:, :128] - from_imag[:, 128:])
        outs[1].append(from_imag[:, :128] + from_real[:, 128:])
    return outs


def turns(angle):
    count = jnp.floor(angle * (2.0 / math.pi) + 0.5)
    rest = ((angle - count * 1.5703125) - count * 4.837512969970703125e-4) - count * 7.54978995489188216e-8
    quadrant = count.astype(jnp.int32)
    square = rest * rest
    sine = rest + rest * square * (-1.6666654611e-1 + square * (8.3321608736e-3 - 1.9515295891e-4 * square))
    cosine = (1.0 - 0.5 * square) + square * square * (
        4.166664568298827e-2 + square * (-1.388731625493765e-3 + 2.443315711809948e-5 * square)
    )
    odd = (quadrant & 1) == 1
    cos_turn = jnp.where(odd, sine, cosine)
    sin_turn = jnp.where(odd, cosine, sine)
    return (
        jnp.where(((quadrant + 1) & 2) == 2, -cos_turn, cos_turn),
        jnp.where((quadrant & 2) == 2, -sin_turn, sin_turn),
    )


def first_kernel(field_hbm, table_hbm, out_ref, field_ref, table_ref, sems):
    copies = [
        pltpu.make_async_copy(field_hbm, field_ref, sems.at[0]),
        pltpu.make_async_copy(table_hbm, table_ref, sems.at[1]),
    ]
    for copy in copies:
        copy.start()
    for copy in copies:
        copy.wait()
    real = field_ref[0]
    imag = field_ref[1]
    reals, imags = along_y(real, imag, table_ref)
    half = NY // 2
    for j in range(2):
        out_ref[pl.ds(3 * half * j, half, stride=3), :] = reals[j]
        out_ref[pl.ds(3 * half * j + 1, half, stride=3), :] = imags[j]
    power = jnp.sum(real * real + imag * imag, axis=0, keepdims=True)
    out_ref[pl.ds(2, NY, stride=3), :] = jnp.broadcast_to(power, (NY, 128))


def time_kernel(in_ref, table_ref, out_ref):
    blocks = [[in_ref[pl.ds(3 * g + p, HALF_X, stride=12), :] for g in range(4)] for p in range(2)]
    outs = along_t(blocks, table_ref)
    for p in range(2):
        for g in range(4):
            out_ref[p * HALF_X : (p + 1) * HALF_X, 128 * g : 128 * (g + 1)] = outs[p][g]
    power = jnp.sum(in_ref[pl.ds(2, NY, stride=3), :], axis=0, keepdims=True)
    out_ref[NX:, :128] = jnp.broadcast_to(power, (8, 128))


def kick_kernel(place_ref, position_ref, mine_ref, other_ref, well_ref, x_table_ref, t_table_ref, out_ref, work_ref):
    core = place_ref[0]
    lower = core == 0
    total = jnp.sum(mine_ref[NX : NX + 1, :128] + other_ref[NX : NX + 1, :128], axis=1, keepdims=True)
    scale = 1.0 / jnp.sqrt(total * (1.0 / (NX * NY * NT)) + EPSILON)
    for p in range(2):
        kept = mine_ref[p * HALF_X : (p + 1) * HALF_X]
        got = other_ref[p * HALF_X : (p + 1) * HALF_X]
        work_ref[p * NX : p * NX + HALF_X] = jnp.where(lower, kept, got)
        work_ref[p * NX + HALF_X : (p + 1) * NX] = jnp.where(lower, got, kept)
    high, low = pieces(work_ref[...])
    for parity in range(2):
        table = x_table_ref[0, parity]
        first = dot(table, high) + (dot(table, low) + dot(x_table_ref[1, parity], high))
        for p in range(2):
            work_ref[p * NX + parity * HALF_X : p * NX + (parity + 1) * HALF_X] = first[p * HALF_X : (p + 1) * HALF_X]
    place_y = (position_ref[place_ref[1]].astype(jnp.float32) - (NY - 1) / 2.0) / (NY / 2.0)
    well_y = WELL * place_y * place_y
    for start in range(0, NX, 8):
        well = jnp.concatenate([well_ref[start : start + 8] + well_y] * 4, axis=1)
        real = work_ref[start : start + 8] * scale
        imag = work_ref[NX + start : NX + start + 8] * scale
        cos_turn, sin_turn = turns(KERR * (real * real + imag * imag) - well)
        work_ref[start : start + 8] = real * cos_turn - imag * sin_turn
        work_ref[NX + start : NX + start + 8] = real * sin_turn + imag * cos_turn
    high, low = pieces(work_ref[...])
    table = x_table_ref[0, core]
    second = dot(table, high) + (dot(table, low) + dot(x_table_ref[1, core], high))
    blocks = [[second[p * HALF_X : (p + 1) * HALF_X, 128 * g : 128 * (g + 1)] for g in range(4)] for p in range(2)]
    outs = along_t(blocks, t_table_ref)
    for p in range(2):
        for g in range(4):
            out_ref[pl.ds(2 * g + p, HALF_X, stride=8), :] = outs[p][g]


def last_kernel(in_ref, table_ref, out_ref):
    real = in_ref[pl.ds(0, NY, stride=2), :]
    imag = in_ref[pl.ds(1, NY, stride=2), :]
    reals, imags = along_y(real, imag, table_ref)
    half = NY // 2
    for j in range(2):
        out_ref[0, j * half : (j + 1) * half] = reals[j]
        out_ref[1, j * half : (j + 1) * half] = imags[j]


def call(kernel, shape, *args, scratch=(), direct=False):
    def place(a):
        if a.dtype == jnp.int32:
            return pltpu.SMEM
        return pltpu.HBM if direct else pltpu.VMEM

    return pl.pallas_call(
        kernel,
        in_specs=[pl.BlockSpec(memory_space=place(a)) for a in args],
        out_specs=pl.BlockSpec(memory_space=pltpu.VMEM),
        out_shape=jax.ShapeDtypeStruct(shape, jnp.float32),
        scratch_shapes=list(scratch),
        compiler_params=pltpu.CompilerParams(vmem_limit_bytes=16 * 2**20),
        name=kernel.__name__,
    )(*args)


def groups():
    return [[run * 8 + core * 4 + t for run in run_order() for t in range(4)] for core in range(2)]


def to_chips(rows, count):
    moved = lax.all_to_all(
        rows.reshape(NY, 1, count * 128),
        DEVICES,
        split_axis=0,
        concat_axis=0,
        tiled=True,
        axis_index_groups=groups(),
    )
    return moved.reshape(count * NY, 128)


def on_device(field, y_table, t_table, x_table, well, positions):
    place = jnp.stack([lax.axis_index("c"), lax.axis_index(CHIPS)]).astype(jnp.int32)
    scratch = [pltpu.VMEM((2, NY, 128), jnp.float32), pltpu.VMEM(y_table.shape, jnp.bfloat16), pltpu.SemaphoreType.DMA((2,))]
    from_hbm = [pltpu.with_memory_space_constraint(a, pltpu.HBM) for a in (field.reshape(2, NY, 128), y_table)]
    rows = call(first_kernel, (3 * NY, 128), *from_hbm, scratch=scratch, direct=True)
    mine = call(time_kernel, (NX + 8, NT), to_chips(rows, 3), t_table)
    other = lax.ppermute(mine, "c", [(0, 1), (1, 0)])
    scratch = [pltpu.VMEM((2 * NX, NT), jnp.float32)]
    rows = call(kick_kernel, (2 * NY, 128), place, positions, mine, other, well, x_table, t_table, scratch=scratch)
    out = call(last_kernel, (2, NY, 128), to_chips(rows, 2), y_table)
    return out.reshape(2, 1, NY, 128)


def solution(mesh):
    torus = Mesh(mesh.devices.reshape(8, 4, 2, 2, mesh.shape["tm"]), DEVICES)
    runs = np.array(run_order())
    order = np.concatenate([2 * runs, 2 * runs + 1])
    positions = np.empty((NY,), np.int32)
    positions[(4 * runs[:, None] + np.arange(4)).reshape(-1)] = np.arange(NY)
    along_x = propagator(NX, -DIFFRACT)
    y_rows = propagator(NY, -DIFFRACT)[: NY // 2]
    t_columns = propagator(NT, DISPERSE).T[:, :128]
    t_columns = np.concatenate([t_columns.real, t_columns.imag], axis=1)
    x_block = real_block(along_x[order][:, order])
    place_x = (order - (NX - 1) / 2.0) / (NX / 2.0)
    tables = (
        split(np.concatenate([y_rows.real, y_rows.imag], axis=0)),
        split(np.concatenate([t_columns[: NT // 2], t_columns[NT // 2 :]], axis=1)),
        x_block.reshape(2, 2, 2, HALF_X, 2 * NX).transpose(0, 2, 1, 3, 4).reshape(2, 2, NX, 2 * NX),
        np.broadcast_to((WELL * place_x**2).astype(np.float32)[:, None], (NX, 128)),
        positions,
    )
    placed = P(None, SLAB, None, "t")
    inner = jax.shard_map(
        lambda field: on_device(field, *[jnp.asarray(table) for table in tables]),
        mesh=torus,
        in_specs=(placed,),
        out_specs=placed,
        check_vma=False,
    )
    return inner
```

time: 71.3 us -> 67.2 us (0.942)
  local copies, waits for them, and re-layouts: 3.6 us -> 0.1 us
  blocking collectives: 58.7 us -> 56.8 us
  Pallas kernels: 4.13 us -> 5.16 us
    unnamed x12 -> x10, local copies, waits for them, and re-layouts: 3.6 us -> 0.03 us
    all_to_all x2, blocking collectives: 58.7 us -> 56.8 us  [to_chips(): lax.all_to_all(rows.reshape(NY, 1, count * 128), DEVICES, split_axis=0, c...]
    pallas_call x4, Pallas kernels: 4.13 us -> 5.16 us  [call(): pl.pallas_call(kernel, in_specs=[pl.BlockSpec(memory_space=place(a)) for...]
where the time goes in v3:
time: 67.2 us; the launch traced here: 66.7 us
  blocking collectives  56.8 us (85%)
  Pallas kernels  5.16 us (8%)
  starting transfers between devices  3.41 us (5%)
  waiting for transfers between devices  1.06 us (2%)
    all_to_all x2, blocking collectives, to_chips(): lax.all_to_all(rows.reshape(NY, 1, count * 128), DEVICES, split_axis=0, c...  56.8 us
    pallas_call x4, Pallas kernels, call(): pl.pallas_call(kernel, in_specs=[pl.BlockSpec(memory_space=place(a)) for...  5.16 us
    ppermute x1, starting transfers between devices, on_device(): other = lax.ppermute(mine, 'c', [(0, 1), (1, 0)])  3.41 us
  transfers between devices with their start and end apart: 1, of which 1 were waited for; matrix products, arithmetic and copies ran while one was open for 0% of the time, Pallas kernels for 0%

profile of v3, /device:TPU:1, one launch (start us, length us, event | category | flops | bytes accessed | tf_op | source)
XLA Modules:
  0.0 66.7 jit_solution(16354962583830973730)
XLA Ops:
  0.0 1.4 %first_kernel.1 = f32[768,128]{1,0:T(8,128)S(1)} custom-call(f32[2,256,128]{2,1,0:T(8,128)} %bitcast.14, bf16[2,256,256]{2,1,0:T(8,128)(2,1)} %constant.37.clone.table_hbm.table_ref), custom_call_target="tpu_custom_call" | custom-call | tf_op jit(solution)/shard_map/first_kernel/pallas_call | solution.py:213
  1.4 0.0 copy-start
  1.4 33.9 %all_to_all.10 = f32[256,1,384]{2,1,0:T(1,128)S(1)} all-to-all(f32[256,1,384]{2,1,0:T(1,128)S(1)} %bitcast.10), channel_id=1, replica_groups={{296,297,298,299,0,1,2,3,16,17,18,19,48,49,50,51,64,65,66,67,448,449,45..., dimensions={0} | all-to-all | bytes 786432 | tf_op jit(solution)/shard_map/all_to_all | solution.py:229
  35.3 0.0 copy-done
  35.3 0.0 copy-start.2
  35.3 0.6 time_kernel.1.mine_ref
  35.9 3.4 %collective-permute-start = (f32[136,512]{1,0:T(8,128)S(1)}, f32[136,512]{1,0:T(8,128)S(1)}, u32[]{:S(2)}, u32[]{:S(2)}) collective-permute-start(f32[136,512]{1,0:T(8,128)S(1)} %time_kernel.1.mine_ref), channel_id=1, source_target_pairs={{0,4},{4,0},{1,5},{5,1},{2,6},{6,2},{3,7},{7,3},{8,12},{12,8},{9,1... | collective-permute-start | bytes 835592 | tf_op jit(solution)/shard_map/ppermute | solution.py:246
  39.3 0.0 copy-start.4
  39.3 0.1 pad_add_fusion.place_ref
  39.4 0.0 copy-start.3
  39.4 1.1 %collective-permute-done.other_ref = f32[136,512]{1,0:T(8,128)S(1)} collective-permute-done((f32[136,512]{1,0:T(8,128)S(1)}, f32[136,512]{1,0:T(8,128)S(1)}, u32[]{:S(2)}, u32[]{:S(2)}) %collective-permute-start) | collective-permute-done | bytes 278560 | tf_op jit(solution)/shard_map/ppermute | solution.py:246
  40.5 0.0 copy-done.4
  40.5 0.1 jit_solution_.3.well_ref
  40.5 0.0 copy-done.2
  40.6 0.0 copy-done.3
  40.6 2.1 %kick_kernel.1 = f32[512,128]{1,0:T(8,128)S(1)} custom-call(s32[2]{0:T(128)S(1)} %pad_add_fusion.place_ref, s32[256]{0:T(256)S(1)} %copy-done.3, f32[136,512]{1,0:T(8,128)S(1)} %time_kernel.1.mine_ref, f32[136,512]{1,0:T(8,128)S(1)} %collective-permute-done.other_ref, f32[128,128]{1,0:T(8,128)S(1)} %jit_solution_.3.well_ref, ...), custom_call_target="tpu_custom_call" | custom-call | tf_op jit(solution)/shard_map/kick_kernel/pallas_call | solution.py:213
  42.7 0.0 copy-start.1
  42.7 23.0 %all_to_all.11 = f32[256,1,256]{2,1,0:T(1,128)S(1)} all-to-all(f32[256,1,256]{2,1,0:T(1,128)S(1)} %bitcast.13), channel_id=1, replica_groups={{296,297,298,299,0,1,2,3,16,17,18,19,48,49,50,51,64,65,66,67,448,449,45..., dimensions={0} | all-to-all | bytes 524288 | tf_op jit(solution)/shard_map/all_to_all | solution.py:229
  65.6 0.0 copy-done.1
  65.6 1.1 %last_kernel.1 = f32[2,256,128]{2,1,0:T(8,128)} custom-call(f32[512,128]{1,0:T(8,128)S(1)} %bitcast.12, bf16[2,256,256]{2,1,0:T(8,128)(2,1)S(1)} %copy-done.1), custom_call_target="tpu_custom_call" | custom-call | tf_op jit(solution)/shard_map/last_kernel/pallas_call | solution.py:213
Async XLA Ops:
  1.4 33.9 %copy-start = (bf16[2,256,512]{2,1,0:T(8,128)(2,1)S(1)}, bf16[2,256,512]{2,1,0:T(8,128)(2,1)}, u32[]{:S(2)}) copy-start(bf16[2,256,512]{2,1,0:T(8,128)(2,1)} %constant.38.clone.table_ref.t_table_ref) | copy-start | bytes 1572868
  35.3 5.2 %copy-start.2 = (bf16[2,2,128,256]{3,2,1,0:T(8,128)(2,1)S(1)}, bf16[2,2,128,256]{3,2,1,0:T(8,128)(2,1)}, u32[]{:S(2)}) copy-start(bf16[2,2,128,256]{3,2,1,0:T(8,128)(2,1)} %constant.39.clone.x_table_ref) | copy-start | bytes 786436
  35.9 4.6 %collective-permute-start = (f32[136,512]{1,0:T(8,128)S(1)}, f32[136,512]{1,0:T(8,128)S(1)}, u32[]{:S(2)}, u32[]{:S(2)}) collective-permute-start(f32[136,512]{1,0:T(8,128)S(1)} %time_kernel.1.mine_ref), channel_id=1, source_target_pairs={{0,4},{4,0},{1,5},{5,1},{2,6},{6,2},{3,7},{7,3},{8,12},{12,8},{9,1... | collective-permute-start | bytes 835592 | tf_op jit(solution)/shard_map/ppermute | solution.py:246
  39.3 1.2 %copy-start.4 = (f32[128]{0:T(128)S(1)}, f32[128]{0:T(128)}, u32[]{:S(2)}) copy-start(f32[128]{0:T(128)} %constant.40.clone) | copy-start | bytes 1540
  39.4 1.2 %copy-start.3 = (s32[256]{0:T(256)S(1)}, s32[256]{0:T(256)}, u32[]{:S(2)}) copy-start(s32[256]{0:T(256)} %constant.41.clone.position_ref) | copy-start | bytes 3076
  42.7 23.0 %copy-start.1 = (bf16[2,256,256]{2,1,0:T(8,128)(2,1)S(1)}, bf16[2,256,256]{2,1,0:T(8,128)(2,1)}, u32[]{:S(2)}) copy-start(bf16[2,256,256]{2,1,0:T(8,128)(2,1)} %constant.37.clone.table_hbm.table_ref) | copy-start | bytes 786436

commit v4 on v3

--- a/solution.py
+++ b/solution.py
@@ -19,7 +19,8 @@
 DEVICES = ("z", "x", "h", "c", "t")
 EXTENT = (8, 4, 8)
 ROOT = (4, 2, 4)
-HOP = (0.46, 0.41, 0.54)
+STEP = 1.02
+HOP = (0.47, 0.45, 0.62)
 
 TWO_PI = 2.0 * math.pi
 DIFFRACT = 4.0
@@ -45,13 +46,12 @@
 
 
 def run_order():
-    def cost(run):
-        place = (run >> 3, (run >> 1) & 3, 4 * (run & 1))
-        away = [abs(p - r) for p, r in zip(place, ROOT)]
-        return sum(w * min(d, n - d) for w, d, n in zip(HOP, away, EXTENT))
+    def start(run):
+        place = (run >> 3, (run >> 1) & 3, 4 * (run & 1) + 1.5)
+        return STEP * place[0] + sum(w * min(p, n - p) for w, p, n in zip(HOP, place, EXTENT))
 
     root = ROOT[0] * 8 + ROOT[1] * 2 + ROOT[2] // 4
-    return [root] + sorted((run for run in range(HALF_X) if run != root), key=lambda run: (-cost(run), run))
+    return [root] + sorted((run for run in range(HALF_X) if run != root), key=lambda run: (-start(run), run))
 
 
 def real_block(matrix):

time: 67.2 us -> 67.8 us (level)
  blocking collectives: 56.8 us -> 58.2 us
    all_to_all x2, blocking collectives: 56.8 us -> 58.2 us  [to_chips(): lax.all_to_all(rows.reshape(NY, 1, count * 128), DEVICES, split_axis=0, c...]
where the time goes in v4:
time: 67.8 us; the launch traced here: 67.5 us
  blocking collectives  58.2 us (86%)
  Pallas kernels  5.17 us (8%)
  starting transfers between devices  2.86 us (4%)
  waiting for transfers between devices  1.06 us (2%)
    all_to_all x2, blocking collectives, to_chips(): lax.all_to_all(rows.reshape(NY, 1, count * 128), DEVICES, split_axis=0, c...  58.2 us
    pallas_call x4, Pallas kernels, call(): pl.pallas_call(kernel, in_specs=[pl.BlockSpec(memory_space=place(a)) for...  5.17 us
    ppermute x1, starting transfers between devices, on_device(): other = lax.ppermute(mine, 'c', [(0, 1), (1, 0)])  2.86 us
  transfers between devices with their start and end apart: 1, of which 1 were waited for; matrix products, arithmetic and copies ran while one was open for 0% of the time, Pallas kernels for 0%

profile of v4, /device:TPU:1, one launch (start us, length us, event | category | flops | bytes accessed | tf_op | source)
XLA Modules:
  0.0 67.5 jit_solution(7311579325502631459)
XLA Ops:
  0.0 1.4 %first_kernel.1 = f32[768,128]{1,0:T(8,128)S(1)} custom-call(f32[2,256,128]{2,1,0:T(8,128)} %bitcast.14, bf16[2,256,256]{2,1,0:T(8,128)(2,1)} %constant.37.clone.table_hbm.table_ref), custom_call_target="tpu_custom_call" | custom-call | tf_op jit(solution)/shard_map/first_kernel/pallas_call | solution.py:213
  1.4 0.0 copy-start
  1.4 34.4 %all_to_all.10 = f32[256,1,384]{2,1,0:T(1,128)S(1)} all-to-all(f32[256,1,384]{2,1,0:T(1,128)S(1)} %bitcast.10), channel_id=1, replica_groups={{296,297,298,299,488,489,490,491,472,473,474,475,504,505,506,507,424,42..., dimensions={0} | all-to-all | bytes 786432 | tf_op jit(solution)/shard_map/all_to_all | solution.py:229
  35.9 0.0 copy-done
  35.9 0.0 copy-start.2
  35.9 0.6 time_kernel.1.mine_ref
  36.4 2.9 %collective-permute-start = (f32[136,512]{1,0:T(8,128)S(1)}, f32[136,512]{1,0:T(8,128)S(1)}, u32[]{:S(2)}, u32[]{:S(2)}) collective-permute-start(f32[136,512]{1,0:T(8,128)S(1)} %time_kernel.1.mine_ref), channel_id=1, source_target_pairs={{0,4},{4,0},{1,5},{5,1},{2,6},{6,2},{3,7},{7,3},{8,12},{12,8},{9,1... | collective-permute-start | bytes 835592 | tf_op jit(solution)/shard_map/ppermute | solution.py:246
  39.3 0.0 copy-start.4
  39.3 0.1 pad_add_fusion.place_ref
  39.4 0.0 copy-start.3
  39.4 1.1 %collective-permute-done.other_ref = f32[136,512]{1,0:T(8,128)S(1)} collective-permute-done((f32[136,512]{1,0:T(8,128)S(1)}, f32[136,512]{1,0:T(8,128)S(1)}, u32[]{:S(2)}, u32[]{:S(2)}) %collective-permute-start) | collective-permute-done | bytes 278560 | tf_op jit(solution)/shard_map/ppermute | solution.py:246
  40.5 0.0 copy-done.4
  40.5 0.1 jit_solution_.3.well_ref
  40.6 0.0 copy-done.2
  40.6 0.0 copy-done.3
  40.6 2.1 %kick_kernel.1 = f32[512,128]{1,0:T(8,128)S(1)} custom-call(s32[2]{0:T(128)S(1)} %pad_add_fusion.place_ref, s32[256]{0:T(256)S(1)} %copy-done.3, f32[136,512]{1,0:T(8,128)S(1)} %time_kernel.1.mine_ref, f32[136,512]{1,0:T(8,128)S(1)} %collective-permute-done.other_ref, f32[128,128]{1,0:T(8,128)S(1)} %jit_solution_.3.well_ref, ...), custom_call_target="tpu_custom_call" | custom-call | tf_op jit(solution)/shard_map/kick_kernel/pallas_call | solution.py:213
  42.7 0.0 copy-start.1
  42.7 23.7 %all_to_all.11 = f32[256,1,256]{2,1,0:T(1,128)S(1)} all-to-all(f32[256,1,256]{2,1,0:T(1,128)S(1)} %bitcast.13), channel_id=1, replica_groups={{296,297,298,299,488,489,490,491,472,473,474,475,504,505,506,507,424,42..., dimensions={0} | all-to-all | bytes 524288 | tf_op jit(solution)/shard_map/all_to_all | solution.py:229
  66.4 0.0 copy-done.1
  66.4 1.1 %last_kernel.1 = f32[2,256,128]{2,1,0:T(8,128)} custom-call(f32[512,128]{1,0:T(8,128)S(1)} %bitcast.12, bf16[2,256,256]{2,1,0:T(8,128)(2,1)S(1)} %copy-done.1), custom_call_target="tpu_custom_call" | custom-call | tf_op jit(solution)/shard_map/last_kernel/pallas_call | solution.py:213
Async XLA Ops:
  1.4 34.4 %copy-start = (bf16[2,256,512]{2,1,0:T(8,128)(2,1)S(1)}, bf16[2,256,512]{2,1,0:T(8,128)(2,1)}, u32[]{:S(2)}) copy-start(bf16[2,256,512]{2,1,0:T(8,128)(2,1)} %constant.38.clone.table_ref.t_table_ref) | copy-start | bytes 1572868
  35.9 4.7 %copy-start.2 = (bf16[2,2,128,256]{3,2,1,0:T(8,128)(2,1)S(1)}, bf16[2,2,128,256]{3,2,1,0:T(8,128)(2,1)}, u32[]{:S(2)}) copy-start(bf16[2,2,128,256]{3,2,1,0:T(8,128)(2,1)} %constant.39.clone.x_table_ref) | copy-start | bytes 786436
  36.4 4.0 %collective-permute-start = (f32[136,512]{1,0:T(8,128)S(1)}, f32[136,512]{1,0:T(8,128)S(1)}, u32[]{:S(2)}, u32[]{:S(2)}) collective-permute-start(f32[136,512]{1,0:T(8,128)S(1)} %time_kernel.1.mine_ref), channel_id=1, source_target_pairs={{0,4},{4,0},{1,5},{5,1},{2,6},{6,2},{3,7},{7,3},{8,12},{12,8},{9,1... | collective-permute-start | bytes 835592 | tf_op jit(solution)/shard_map/ppermute | solution.py:246
  39.3 1.2 %copy-start.4 = (f32[128]{0:T(128)S(1)}, f32[128]{0:T(128)}, u32[]{:S(2)}) copy-start(f32[128]{0:T(128)} %constant.40.clone) | copy-start | bytes 1540
  39.4 1.2 %copy-start.3 = (s32[256]{0:T(256)S(1)}, s32[256]{0:T(256)}, u32[]{:S(2)}) copy-start(s32[256]{0:T(256)} %constant.41.clone.position_ref) | copy-start | bytes 3076
  42.7 23.8 %copy-start.1 = (bf16[2,256,256]{2,1,0:T(8,128)(2,1)S(1)}, bf16[2,256,256]{2,1,0:T(8,128)(2,1)}, u32[]{:S(2)}) copy-start(bf16[2,256,256]{2,1,0:T(8,128)(2,1)} %constant.37.clone.table_hbm.table_ref) | copy-start | bytes 786436

commit v5 on v4

--- a/solution.py
+++ b/solution.py
@@ -17,10 +17,8 @@
 SLAB = ("z", "x", "h", "c")
 CHIPS = ("z", "x", "h", "t")
 DEVICES = ("z", "x", "h", "c", "t")
-EXTENT = (8, 4, 8)
-ROOT = (4, 2, 4)
-STEP = 1.02
-HOP = (0.47, 0.45, 0.62)
+FLIP_X = 37
+FLIP = 4 * FLIP_X
 
 TWO_PI = 2.0 * math.pi
 DIFFRACT = 4.0
@@ -43,15 +41,6 @@
     high = full.astype(ml_dtypes.bfloat16)
     low = (matrix - high.astype(np.float64)).astype(ml_dtypes.bfloat16)
     return np.stack([high, low])
-
-
-def run_order():
-    def start(run):
-        place = (run >> 3, (run >> 1) & 3, 4 * (run & 1) + 1.5)
-        return STEP * place[0] + sum(w * min(p, n - p) for w, p, n in zip(HOP, place, EXTENT))
-
-    root = ROOT[0] * 8 + ROOT[1] * 2 + ROOT[2] // 4
-    return [root] + sorted((run for run in range(HALF_X) if run != root), key=lambda run: (-start(run), run))
 
 
 def real_block(matrix):
@@ -130,10 +119,10 @@
 
 
 def first_kernel(field_hbm, table_hbm, out_ref, field_ref, table_ref, sems):
-    copies = [
-        pltpu.make_async_copy(field_hbm, field_ref, sems.at[0]),
-        pltpu.make_async_copy(table_hbm, table_ref, sems.at[1]),
-    ]
+    copies = []
+    for p in range(2):
+        copies.append(pltpu.make_async_copy(field_hbm.at[p], field_ref.at[p], sems.at[2 * p]))
+        copies.append(pltpu.make_async_copy(table_hbm.at[p], table_ref.at[p], sems.at[2 * p + 1]))
     for copy in copies:
         copy.start()
     for copy in copies:
@@ -159,35 +148,51 @@
     out_ref[NX:, :128] = jnp.broadcast_to(power, (8, 128))
 
 
-def kick_kernel(place_ref, position_ref, mine_ref, other_ref, well_ref, x_table_ref, t_table_ref, out_ref, work_ref):
-    core = place_ref[0]
-    lower = core == 0
+def kick_kernel(mine_ref, other_ref, x_table_ref, t_table_ref, out_ref):
+    core = lax.axis_index("c")
+    place_y = ((lax.axis_index(CHIPS) ^ FLIP).astype(jnp.float32) - (NY - 1) / 2.0) / (NY / 2.0)
+    well_y = WELL * place_y * place_y
     total = jnp.sum(mine_ref[NX : NX + 1, :128] + other_ref[NX : NX + 1, :128], axis=1, keepdims=True)
     scale = 1.0 / jnp.sqrt(total * (1.0 / (NX * NY * NT)) + EPSILON)
-    for p in range(2):
-        kept = mine_ref[p * HALF_X : (p + 1) * HALF_X]
-        got = other_ref[p * HALF_X : (p + 1) * HALF_X]
-        work_ref[p * NX : p * NX + HALF_X] = jnp.where(lower, kept, got)
-        work_ref[p * NX + HALF_X : (p + 1) * NX] = jnp.where(lower, got, kept)
-    high, low = pieces(work_ref[...])
-    for parity in range(2):
-        table = x_table_ref[0, parity]
-        first = dot(table, high) + (dot(table, low) + dot(x_table_ref[1, parity], high))
-        for p in range(2):
-            work_ref[p * NX + parity * HALF_X : p * NX + (parity + 1) * HALF_X] = first[p * HALF_X : (p + 1) * HALF_X]
-    place_y = (position_ref[place_ref[1]].astype(jnp.float32) - (NY - 1) / 2.0) / (NY / 2.0)
-    well_y = WELL * place_y * place_y
-    for start in range(0, NX, 8):
-        well = jnp.concatenate([well_ref[start : start + 8] + well_y] * 4, axis=1)
-        real = work_ref[start : start + 8] * scale
-        imag = work_ref[NX + start : NX + start + 8] * scale
-        cos_turn, sin_turn = turns(KERR * (real * real + imag * imag) - well)
-        work_ref[start : start + 8] = real * cos_turn - imag * sin_turn
-        work_ref[NX + start : NX + start + 8] = real * sin_turn + imag * cos_turn
-    high, low = pieces(work_ref[...])
     table = x_table_ref[0, core]
-    second = dot(table, high) + (dot(table, low) + dot(x_table_ref[1, core], high))
-    blocks = [[second[p * HALF_X : (p + 1) * HALF_X, 128 * g : 128 * (g + 1)] for g in range(4)] for p in range(2)]
+    table_low = x_table_ref[1, core]
+    own, own_low = [jnp.concatenate([t[:HALF_X], t[NX : NX + HALF_X]], axis=0) for t in (table, table_low)]
+    width = NT // 2
+    row = lax.broadcasted_iota(jnp.int32, (8, width), 0)
+
+    def along_x(b):
+        parts = [
+            ref[p * HALF_X : (p + 1) * HALF_X, b * width : (b + 1) * width]
+            for p in range(2)
+            for ref in (mine_ref, other_ref)
+        ]
+        high, low = pieces(jnp.concatenate(parts, axis=0))
+        return dot(table, high) + (dot(table, low) + dot(table_low, high))
+
+    def kick(first):
+        reals = []
+        imags = []
+        for start in range(0, NX, 8):
+            parity = core if start < HALF_X else 1 - core
+            x = 2 * ((start % HALF_X + row) ^ FLIP_X) + parity
+            place_x = (x.astype(jnp.float32) - (NX - 1) / 2.0) / (NX / 2.0)
+            real = first[start : start + 8] * scale
+            imag = first[NX + start : NX + start + 8] * scale
+            cos_turn, sin_turn = turns(KERR * (real * real + imag * imag) - (WELL * place_x * place_x + well_y))
+            reals.append(real * cos_turn - imag * sin_turn)
+            imags.append(real * sin_turn + imag * cos_turn)
+        return jnp.concatenate(reals + imags, axis=0)
+
+    def along_x_own(kicked):
+        high, low = pieces(kicked)
+        return dot(own, high) + (dot(own, low) + dot(own_low, high))
+
+    firsts = [along_x(0), along_x(1)]
+    seconds = [along_x_own(kick(first)) for first in firsts]
+    blocks = [
+        [seconds[g // 2][p * HALF_X : (p + 1) * HALF_X, 128 * (g % 2) : 128 * (g % 2 + 1)] for g in range(4)]
+        for p in range(2)
+    ]
     outs = along_t(blocks, t_table_ref)
     for p in range(2):
         for g in range(4):
@@ -205,14 +210,10 @@
 
 
 def call(kernel, shape, *args, scratch=(), direct=False):
-    def place(a):
-        if a.dtype == jnp.int32:
-            return pltpu.SMEM
-        return pltpu.HBM if direct else pltpu.VMEM
-
+    source = pltpu.HBM if direct else pltpu.VMEM
     return pl.pallas_call(
         kernel,
-        in_specs=[pl.BlockSpec(memory_space=place(a)) for a in args],
+        in_specs=[pl.BlockSpec(memory_space=source) for _ in args],
         out_specs=pl.BlockSpec(memory_space=pltpu.VMEM),
         out_shape=jax.ShapeDtypeStruct(shape, jnp.float32),
         scratch_shapes=list(scratch),
@@ -222,7 +223,8 @@
 
 
 def groups():
-    return [[run * 8 + core * 4 + t for run in run_order() for t in range(4)] for core in range(2)]
+    chips = [position ^ FLIP for position in range(NY)]
+    return [[(chip >> 2) * 8 + core * 4 + (chip & 3) for chip in chips] for core in range(2)]
 
 
 def to_chips(rows, count):
@@ -237,37 +239,32 @@
     return moved.reshape(count * NY, 128)
 
 
-def on_device(field, y_table, t_table, x_table, well, positions):
-    place = jnp.stack([lax.axis_index("c"), lax.axis_index(CHIPS)]).astype(jnp.int32)
-    scratch = [pltpu.VMEM((2, NY, 128), jnp.float32), pltpu.VMEM(y_table.shape, jnp.bfloat16), pltpu.SemaphoreType.DMA((2,))]
+def on_device(field, y_table, t_table, x_table):
+    scratch = [pltpu.VMEM((2, NY, 128), jnp.float32), pltpu.VMEM(y_table.shape, jnp.bfloat16), pltpu.SemaphoreType.DMA((4,))]
     from_hbm = [pltpu.with_memory_space_constraint(a, pltpu.HBM) for a in (field.reshape(2, NY, 128), y_table)]
     rows = call(first_kernel, (3 * NY, 128), *from_hbm, scratch=scratch, direct=True)
     mine = call(time_kernel, (NX + 8, NT), to_chips(rows, 3), t_table)
     other = lax.ppermute(mine, "c", [(0, 1), (1, 0)])
-    scratch = [pltpu.VMEM((2 * NX, NT), jnp.float32)]
-    rows = call(kick_kernel, (2 * NY, 128), place, positions, mine, other, well, x_table, t_table, scratch=scratch)
+    rows = call(kick_kernel, (2 * NY, 128), mine, other, x_table, t_table)
     out = call(last_kernel, (2, NY, 128), to_chips(rows, 2), y_table)
     return out.reshape(2, 1, NY, 128)
 
 
 def solution(mesh):
     torus = Mesh(mesh.devices.reshape(8, 4, 2, 2, mesh.shape["tm"]), DEVICES)
-    runs = np.array(run_order())
-    order = np.concatenate([2 * runs, 2 * runs + 1])
-    positions = np.empty((NY,), np.int32)
-    positions[(4 * runs[:, None] + np.arange(4)).reshape(-1)] = np.arange(NY)
     along_x = propagator(NX, -DIFFRACT)
+    runs = np.arange(HALF_X) ^ FLIP_X
+    x_tables = []
+    for core in range(2):
+        order = np.concatenate([2 * runs + core, 2 * runs + 1 - core])
+        x_tables.append(real_block(along_x[order][:, order]))
     y_rows = propagator(NY, -DIFFRACT)[: NY // 2]
     t_columns = propagator(NT, DISPERSE).T[:, :128]
     t_columns = np.concatenate([t_columns.real, t_columns.imag], axis=1)
-    x_block = real_block(along_x[order][:, order])
-    place_x = (order - (NX - 1) / 2.0) / (NX / 2.0)
     tables = (
         split(np.concatenate([y_rows.real, y_rows.imag], axis=0)),
         split(np.concatenate([t_columns[: NT // 2], t_columns[NT // 2 :]], axis=1)),
-        x_block.reshape(2, 2, 2, HALF_X, 2 * NX).transpose(0, 2, 1, 3, 4).reshape(2, 2, NX, 2 * NX),
-        np.broadcast_to((WELL * place_x**2).astype(np.float32)[:, None], (NX, 128)),
-        positions,
+        np.stack(x_tables, axis=1),
     )
     placed = P(None, SLAB, None, "t")
     inner = jax.shard_map(

time: 67.8 us -> 68.2 us (level)
  blocking collectives: 58.2 us -> 58.9 us
    all_to_all x2, blocking collectives: 58.2 us -> 58.9 us  [to_chips(): lax.all_to_all(rows.reshape(NY, 1, count * 128), DEVICES, split_axis=0, c...]
where the time goes in v5:
time: 68.2 us; the launch traced here: 68 us
  blocking collectives  58.9 us (86%)
  Pallas kernels  4.75 us (7%)
  starting transfers between devices  3.13 us (5%)
  waiting for transfers between devices  1.16 us (2%)
    all_to_all x2, blocking collectives, to_chips(): lax.all_to_all(rows.reshape(NY, 1, count * 128), DEVICES, split_axis=0, c...  58.9 us
    pallas_call x4, Pallas kernels, call(): pl.pallas_call(kernel, in_specs=[pl.BlockSpec(memory_space=source) for _...  4.75 us
    ppermute x1, starting transfers between devices, on_device(): other = lax.ppermute(mine, 'c', [(0, 1), (1, 0)])  3.13 us
  transfers between devices with their start and end apart: 1, of which 1 were waited for; matrix products, arithmetic and copies ran while one was open for 0% of the time, Pallas kernels for 0%

profile of v5, /device:TPU:1, one launch (start us, length us, event | category | flops | bytes accessed | tf_op | source)
XLA Modules:
  0.0 68.0 jit_solution(11613576210812883750)
XLA Ops:
  0.0 1.5 %first_kernel.1 = f32[768,128]{1,0:T(8,128)S(1)} custom-call(f32[2,256,128]{2,1,0:T(8,128)} %bitcast.12, bf16[2,256,256]{2,1,0:T(8,128)(2,1)} %constant.6.clone.table_hbm.table_ref), custom_call_target="tpu_custom_call" | custom-call | tf_op jit(solution)/shard_map/first_kernel/pallas_call | solution.py:214
  1.5 0.0 copy-start
  1.5 34.3 %all_to_all.10 = f32[256,1,384]{2,1,0:T(1,128)S(1)} all-to-all(f32[256,1,384]{2,1,0:T(1,128)S(1)} %bitcast.8), channel_id=1, replica_groups={{296,297,298,299,288,289,290,291,312,313,314,315,304,305,306,307,264,26..., dimensions={0} | all-to-all | bytes 786432 | tf_op jit(solution)/shard_map/all_to_all | solution.py:231
  35.8 0.0 copy-done
  35.8 0.0 copy-start.2
  35.8 0.6 time_kernel.1.mine_ref
  36.4 3.1 %collective-permute-start = (f32[136,512]{1,0:T(8,128)S(1)}, f32[136,512]{1,0:T(8,128)S(1)}, u32[]{:S(2)}, u32[]{:S(2)}) collective-permute-start(f32[136,512]{1,0:T(8,128)S(1)} %time_kernel.1.mine_ref), channel_id=1, source_target_pairs={{0,4},{4,0},{1,5},{5,1},{2,6},{6,2},{3,7},{7,3},{8,12},{12,8},{9,1... | collective-permute-start | bytes 835592 | tf_op jit(solution)/shard_map/ppermute | solution.py:247
  39.5 1.2 %collective-permute-done.other_ref = f32[136,512]{1,0:T(8,128)S(1)} collective-permute-done((f32[136,512]{1,0:T(8,128)S(1)}, f32[136,512]{1,0:T(8,128)S(1)}, u32[]{:S(2)}, u32[]{:S(2)}) %collective-permute-start) | collective-permute-done | bytes 278560 | tf_op jit(solution)/shard_map/ppermute | solution.py:247
  40.7 0.0 copy-done.2
  40.7 1.6 %kick_kernel.1 = f32[512,128]{1,0:T(8,128)S(1)} custom-call(f32[136,512]{1,0:T(8,128)S(1)} %time_kernel.1.mine_ref, f32[136,512]{1,0:T(8,128)S(1)} %collective-permute-done.other_ref, bf16[2,2,256,256]{3,2,1,0:T(8,128)(2,1)S(1)} %copy-done.2, bf16[2,256,512]{2,1,0:T(8,128)(2,1)S(1)} %copy-done), custom_call_target="tpu_custom_call" | custom-call | tf_op jit(solution)/shard_map/kick_kernel/pallas_call | solution.py:214
  42.3 0.0 copy-start.1
  42.3 24.6 %all_to_all.11 = f32[256,1,256]{2,1,0:T(1,128)S(1)} all-to-all(f32[256,1,256]{2,1,0:T(1,128)S(1)} %bitcast.10), channel_id=1, replica_groups={{296,297,298,299,288,289,290,291,312,313,314,315,304,305,306,307,264,26..., dimensions={0} | all-to-all | bytes 524288 | tf_op jit(solution)/shard_map/all_to_all | solution.py:231
  66.9 0.0 copy-done.1
  66.9 1.1 %last_kernel.1 = f32[2,256,128]{2,1,0:T(8,128)} custom-call(f32[512,128]{1,0:T(8,128)S(1)} %bitcast.11, bf16[2,256,256]{2,1,0:T(8,128)(2,1)S(1)} %copy-done.1), custom_call_target="tpu_custom_call" | custom-call | tf_op jit(solution)/shard_map/last_kernel/pallas_call | solution.py:214
Async XLA Ops:
  1.5 34.3 %copy-start = (bf16[2,256,512]{2,1,0:T(8,128)(2,1)S(1)}, bf16[2,256,512]{2,1,0:T(8,128)(2,1)}, u32[]{:S(2)}) copy-start(bf16[2,256,512]{2,1,0:T(8,128)(2,1)} %constant.7.clone.table_ref.t_table_ref) | copy-start | bytes 1572868
  35.8 4.9 %copy-start.2 = (bf16[2,2,256,256]{3,2,1,0:T(8,128)(2,1)S(1)}, bf16[2,2,256,256]{3,2,1,0:T(8,128)(2,1)}, u32[]{:S(2)}) copy-start(bf16[2,2,256,256]{3,2,1,0:T(8,128)(2,1)} %constant.8.clone.x_table_ref) | copy-start | bytes 1572868
  36.4 4.3 %collective-permute-start = (f32[136,512]{1,0:T(8,128)S(1)}, f32[136,512]{1,0:T(8,128)S(1)}, u32[]{:S(2)}, u32[]{:S(2)}) collective-permute-start(f32[136,512]{1,0:T(8,128)S(1)} %time_kernel.1.mine_ref), channel_id=1, source_target_pairs={{0,4},{4,0},{1,5},{5,1},{2,6},{6,2},{3,7},{7,3},{8,12},{12,8},{9,1... | collective-permute-start | bytes 835592 | tf_op jit(solution)/shard_map/ppermute | solution.py:247
  42.3 24.6 %copy-start.1 = (bf16[2,256,256]{2,1,0:T(8,128)(2,1)S(1)}, bf16[2,256,256]{2,1,0:T(8,128)(2,1)}, u32[]{:S(2)}) copy-start(bf16[2,256,256]{2,1,0:T(8,128)(2,1)} %constant.6.clone.table_hbm.table_ref) | copy-start | bytes 786436

commit v6 on v5

--- a/solution.py
+++ b/solution.py
@@ -15,10 +15,10 @@
 NT = 512
 HALF_X = NX // 2
 SLAB = ("z", "x", "h", "c")
-CHIPS = ("z", "x", "h", "t")
 DEVICES = ("z", "x", "h", "c", "t")
-FLIP_X = 37
-FLIP = 4 * FLIP_X
+RUN_BITS = (5, 4, 3, 2, 1, 0)
+FLIP = 37
+T_HIGH = True
 
 TWO_PI = 2.0 * math.pi
 DIFFRACT = 4.0
@@ -41,6 +41,25 @@
     high = full.astype(ml_dtypes.bfloat16)
     low = (matrix - high.astype(np.float64)).astype(ml_dtypes.bfloat16)
     return np.stack([high, low])
+
+
+def spread(place):
+    return sum(((place >> i) & 1) << bit for i, bit in enumerate(RUN_BITS))
+
+
+def run_at(place):
+    return spread(place) ^ FLIP
+
+
+def position_of(run, t):
+    place = sum((((run ^ FLIP) >> bit) & 1) << i for i, bit in enumerate(RUN_BITS))
+    return t * HALF_X + place if T_HIGH else 4 * place + t
+
+
+def rows_of(t, part, count):
+    if T_HIGH:
+        return pl.ds(count * HALF_X * t + part, HALF_X, stride=count)
+    return pl.ds(count * t + part, HALF_X, stride=4 * count)
 
 
 def real_block(matrix):
@@ -119,10 +138,10 @@
 
 
 def first_kernel(field_hbm, table_hbm, out_ref, field_ref, table_ref, sems):
-    copies = []
-    for p in range(2):
-        copies.append(pltpu.make_async_copy(field_hbm.at[p], field_ref.at[p], sems.at[2 * p]))
-        copies.append(pltpu.make_async_copy(table_hbm.at[p], table_ref.at[p], sems.at[2 * p + 1]))
+    copies = [
+        pltpu.make_async_copy(field_hbm, field_ref, sems.at[0]),
+        pltpu.make_async_copy(table_hbm, table_ref, sems.at[1]),
+    ]
     for copy in copies:
         copy.start()
     for copy in copies:
@@ -139,7 +158,7 @@
 
 
 def time_kernel(in_ref, table_ref, out_ref):
-    blocks = [[in_ref[pl.ds(3 * g + p, HALF_X, stride=12), :] for g in range(4)] for p in range(2)]
+    blocks = [[in_ref[rows_of(g, p, 3), :] for g in range(4)] for p in range(2)]
     outs = along_t(blocks, table_ref)
     for p in range(2):
         for g in range(4):
@@ -150,7 +169,8 @@
 
 def kick_kernel(mine_ref, other_ref, x_table_ref, t_table_ref, out_ref):
     core = lax.axis_index("c")
-    place_y = ((lax.axis_index(CHIPS) ^ FLIP).astype(jnp.float32) - (NY - 1) / 2.0) / (NY / 2.0)
+    position = position_of(lax.axis_index(("z", "x", "h")), lax.axis_index("t"))
+    place_y = (position.astype(jnp.float32) - (NY - 1) / 2.0) / (NY / 2.0)
     well_y = WELL * place_y * place_y
     total = jnp.sum(mine_ref[NX : NX + 1, :128] + other_ref[NX : NX + 1, :128], axis=1, keepdims=True)
     scale = 1.0 / jnp.sqrt(total * (1.0 / (NX * NY * NT)) + EPSILON)
@@ -158,7 +178,7 @@
     table_low = x_table_ref[1, core]
     own, own_low = [jnp.concatenate([t[:HALF_X], t[NX : NX + HALF_X]], axis=0) for t in (table, table_low)]
     width = NT // 2
-    row = lax.broadcasted_iota(jnp.int32, (8, width), 0)
+    low_run = spread(lax.broadcasted_iota(jnp.int32, (8, width), 0))
 
     def along_x(b):
         parts = [
@@ -174,7 +194,7 @@
         imags = []
         for start in range(0, NX, 8):
             parity = core if start < HALF_X else 1 - core
-            x = 2 * ((start % HALF_X + row) ^ FLIP_X) + parity
+            x = 2 * (low_run ^ run_at(start % HALF_X)) + parity
             place_x = (x.astype(jnp.float32) - (NX - 1) / 2.0) / (NX / 2.0)
             real = first[start : start + 8] * scale
             imag = first[NX + start : NX + start + 8] * scale
@@ -196,7 +216,7 @@
     outs = along_t(blocks, t_table_ref)
     for p in range(2):
         for g in range(4):
-            out_ref[pl.ds(2 * g + p, HALF_X, stride=8), :] = outs[p][g]
+            out_ref[rows_of(g, p, 2), :] = outs[p][g]
 
 
 def last_kernel(in_ref, table_ref, out_ref):
@@ -223,8 +243,12 @@
 
 
 def groups():
-    chips = [position ^ FLIP for position in range(NY)]
-    return [[(chip >> 2) * 8 + core * 4 + (chip & 3) for chip in chips] for core in range(2)]
+    found = np.empty((2, NY), np.int64)
+    for run in range(HALF_X):
+        for t in range(4):
+            for core in range(2):
+                found[core, position_of(run, t)] = run * 8 + core * 4 + t
+    return found.tolist()
 
 
 def to_chips(rows, count):
@@ -240,7 +264,7 @@
 
 
 def on_device(field, y_table, t_table, x_table):
-    scratch = [pltpu.VMEM((2, NY, 128), jnp.float32), pltpu.VMEM(y_table.shape, jnp.bfloat16), pltpu.SemaphoreType.DMA((4,))]
+    scratch = [pltpu.VMEM((2, NY, 128), jnp.float32), pltpu.VMEM(y_table.shape, jnp.bfloat16), pltpu.SemaphoreType.DMA((2,))]
     from_hbm = [pltpu.with_memory_space_constraint(a, pltpu.HBM) for a in (field.reshape(2, NY, 128), y_table)]
     rows = call(first_kernel, (3 * NY, 128), *from_hbm, scratch=scratch, direct=True)
     mine = call(time_kernel, (NX + 8, NT), to_chips(rows, 3), t_table)
@@ -253,7 +277,7 @@
 def solution(mesh):
     torus = Mesh(mesh.devices.reshape(8, 4, 2, 2, mesh.shape["tm"]), DEVICES)
     along_x = propagator(NX, -DIFFRACT)
-    runs = np.arange(HALF_X) ^ FLIP_X
+    runs = run_at(np.arange(HALF_X))
     x_tables = []
     for core in range(2):
         order = np.concatenate([2 * runs + core, 2 * runs + 1 - core])

time: 68.2 us -> 65.8 us (0.965)
  blocking collectives: 58.9 us -> 56.3 us
    all_to_all x2, blocking collectives: 58.9 us -> 56.3 us  [to_chips(): lax.all_to_all(rows.reshape(NY, 1, count * 128), DEVICES, split_axis=0, c...]
where the time goes in v6:
time: 65.8 us; the launch traced here: 65.5 us
  blocking collectives  56.3 us (86%)
  Pallas kernels  4.66 us (7%)
  starting transfers between devices  3.3 us (5%)
  waiting for transfers between devices  1.16 us (2%)
    all_to_all x2, blocking collectives, to_chips(): lax.all_to_all(rows.reshape(NY, 1, count * 128), DEVICES, split_axis=0, c...  56.3 us
    pallas_call x4, Pallas kernels, call(): pl.pallas_call(kernel, in_specs=[pl.BlockSpec(memory_space=source) for _...  4.66 us
    ppermute x1, starting transfers between devices, on_device(): other = lax.ppermute(mine, 'c', [(0, 1), (1, 0)])  3.3 us
  transfers between devices with their start and end apart: 1, of which 1 were waited for; matrix products, arithmetic and copies ran while one was open for 0% of the time, Pallas kernels for 0%

profile of v6, /device:TPU:1, one launch (start us, length us, event | category | flops | bytes accessed | tf_op | source)
XLA Modules:
  0.0 65.5 jit_solution(11204598923815208074)
XLA Ops:
  0.0 1.4 %first_kernel.1 = f32[768,128]{1,0:T(8,128)S(1)} custom-call(f32[2,256,128]{2,1,0:T(8,128)} %bitcast.12, bf16[2,256,256]{2,1,0:T(8,128)(2,1)} %constant.6.clone.table_hbm.table_ref), custom_call_target="tpu_custom_call" | custom-call | tf_op jit(solution)/shard_map/first_kernel/pallas_call | solution.py:234
  1.4 0.0 copy-start
  1.4 33.9 %all_to_all.10 = f32[256,1,384]{2,1,0:T(1,128)S(1)} all-to-all(f32[256,1,384]{2,1,0:T(1,128)S(1)} %bitcast.8), channel_id=1, replica_groups={{296,40,424,168,360,104,488,232,264,8,392,136,328,72,456,200,312,56,440..., dimensions={0} | all-to-all | bytes 786432 | tf_op jit(solution)/shard_map/all_to_all | solution.py:255
  35.3 0.0 copy-done
  35.3 0.0 copy-start.2
  35.3 0.6 time_kernel.1.mine_ref
  35.9 3.3 %collective-permute-start = (f32[136,512]{1,0:T(8,128)S(1)}, f32[136,512]{1,0:T(8,128)S(1)}, u32[]{:S(2)}, u32[]{:S(2)}) collective-permute-start(f32[136,512]{1,0:T(8,128)S(1)} %time_kernel.1.mine_ref), channel_id=1, source_target_pairs={{0,4},{4,0},{1,5},{5,1},{2,6},{6,2},{3,7},{7,3},{8,12},{12,8},{9,1... | collective-permute-start | bytes 835592 | tf_op jit(solution)/shard_map/ppermute | solution.py:271
  39.2 1.2 %collective-permute-done.other_ref = f32[136,512]{1,0:T(8,128)S(1)} collective-permute-done((f32[136,512]{1,0:T(8,128)S(1)}, f32[136,512]{1,0:T(8,128)S(1)}, u32[]{:S(2)}, u32[]{:S(2)}) %collective-permute-start) | collective-permute-done | bytes 278560 | tf_op jit(solution)/shard_map/ppermute | solution.py:271
  40.4 0.0 copy-done.2
  40.4 1.6 %kick_kernel.1 = f32[512,128]{1,0:T(8,128)S(1)} custom-call(f32[136,512]{1,0:T(8,128)S(1)} %time_kernel.1.mine_ref, f32[136,512]{1,0:T(8,128)S(1)} %collective-permute-done.other_ref, bf16[2,2,256,256]{3,2,1,0:T(8,128)(2,1)S(1)} %copy-done.2, bf16[2,256,512]{2,1,0:T(8,128)(2,1)S(1)} %copy-done), custom_call_target="tpu_custom_call" | custom-call | tf_op jit(solution)/shard_map/kick_kernel/pallas_call | solution.py:234
  42.0 0.0 copy-start.1
  42.0 22.4 %all_to_all.11 = f32[256,1,256]{2,1,0:T(1,128)S(1)} all-to-all(f32[256,1,256]{2,1,0:T(1,128)S(1)} %bitcast.10), channel_id=1, replica_groups={{296,40,424,168,360,104,488,232,264,8,392,136,328,72,456,200,312,56,440..., dimensions={0} | all-to-all | bytes 524288 | tf_op jit(solution)/shard_map/all_to_all | solution.py:255
  64.4 0.0 copy-done.1
  64.4 1.1 %last_kernel.1 = f32[2,256,128]{2,1,0:T(8,128)} custom-call(f32[512,128]{1,0:T(8,128)S(1)} %bitcast.11, bf16[2,256,256]{2,1,0:T(8,128)(2,1)S(1)} %copy-done.1), custom_call_target="tpu_custom_call" | custom-call | tf_op jit(solution)/shard_map/last_kernel/pallas_call | solution.py:234
Async XLA Ops:
  1.4 33.9 %copy-start = (bf16[2,256,512]{2,1,0:T(8,128)(2,1)S(1)}, bf16[2,256,512]{2,1,0:T(8,128)(2,1)}, u32[]{:S(2)}) copy-start(bf16[2,256,512]{2,1,0:T(8,128)(2,1)} %constant.7.clone.table_ref.t_table_ref) | copy-start | bytes 1572868
  35.3 5.1 %copy-start.2 = (bf16[2,2,256,256]{3,2,1,0:T(8,128)(2,1)S(1)}, bf16[2,2,256,256]{3,2,1,0:T(8,128)(2,1)}, u32[]{:S(2)}) copy-start(bf16[2,2,256,256]{3,2,1,0:T(8,128)(2,1)} %constant.8.clone.x_table_ref) | copy-start | bytes 1572868
  35.9 4.5 %collective-permute-start = (f32[136,512]{1,0:T(8,128)S(1)}, f32[136,512]{1,0:T(8,128)S(1)}, u32[]{:S(2)}, u32[]{:S(2)}) collective-permute-start(f32[136,512]{1,0:T(8,128)S(1)} %time_kernel.1.mine_ref), channel_id=1, source_target_pairs={{0,4},{4,0},{1,5},{5,1},{2,6},{6,2},{3,7},{7,3},{8,12},{12,8},{9,1... | collective-permute-start | bytes 835592 | tf_op jit(solution)/shard_map/ppermute | solution.py:271
  42.0 22.4 %copy-start.1 = (bf16[2,256,256]{2,1,0:T(8,128)(2,1)S(1)}, bf16[2,256,256]{2,1,0:T(8,128)(2,1)}, u32[]{:S(2)}) copy-start(bf16[2,256,256]{2,1,0:T(8,128)(2,1)} %constant.6.clone.table_hbm.table_ref) | copy-start | bytes 786436

commit v7 on v6

--- a/solution.py
+++ b/solution.py
@@ -119,22 +119,18 @@
     return outs
 
 
-def turns(angle):
-    count = jnp.floor(angle * (2.0 / math.pi) + 0.5)
-    rest = ((angle - count * 1.5703125) - count * 4.837512969970703125e-4) - count * 7.54978995489188216e-8
-    quadrant = count.astype(jnp.int32)
+def turns(half):
+    count = jnp.floor(half * (1.0 / math.pi) + 0.5)
+    rest = ((half - count * 3.140625) - count * 9.67502593994140625e-4) - count * 1.509957990978376432e-7
     square = rest * rest
-    sine = rest + rest * square * (-1.6666654611e-1 + square * (8.3321608736e-3 - 1.9515295891e-4 * square))
-    cosine = (1.0 - 0.5 * square) + square * square * (
-        4.166664568298827e-2 + square * (-1.388731625493765e-3 + 2.443315711809948e-5 * square)
-    )
-    odd = (quadrant & 1) == 1
-    cos_turn = jnp.where(odd, sine, cosine)
-    sin_turn = jnp.where(odd, cosine, sine)
-    return (
-        jnp.where(((quadrant + 1) & 2) == 2, -cos_turn, cos_turn),
-        jnp.where((quadrant & 2) == 2, -sin_turn, sin_turn),
-    )
+    sine = rest + (rest * square) * (
+        -1.66666563e-1 + square * (8.33299813e-3 + square * (-1.98052344e-4 + square * 2.59701156e-6))
+    )
+    cosine = 1.0 + square * (
+        -4.99999268e-1 + square * (4.16638274e-2 + square * (-1.38546172e-3 + square * 2.31630858e-5))
+    )
+    twice = sine + sine
+    return 1.0 - twice * sine, twice * cosine
 
 
 def first_kernel(field_hbm, table_hbm, out_ref, field_ref, table_ref, sems):
@@ -171,14 +167,20 @@
     core = lax.axis_index("c")
     position = position_of(lax.axis_index(("z", "x", "h")), lax.axis_index("t"))
     place_y = (position.astype(jnp.float32) - (NY - 1) / 2.0) / (NY / 2.0)
-    well_y = WELL * place_y * place_y
     total = jnp.sum(mine_ref[NX : NX + 1, :128] + other_ref[NX : NX + 1, :128], axis=1, keepdims=True)
     scale = 1.0 / jnp.sqrt(total * (1.0 / (NX * NY * NT)) + EPSILON)
     table = x_table_ref[0, core]
     table_low = x_table_ref[1, core]
     own, own_low = [jnp.concatenate([t[:HALF_X], t[NX : NX + HALF_X]], axis=0) for t in (table, table_low)]
     width = NT // 2
-    low_run = spread(lax.broadcasted_iota(jnp.int32, (8, width), 0))
+    half_kerr = (0.5 * KERR) * scale * scale
+    low_run = spread(lax.broadcasted_iota(jnp.int32, (8, 128), 0))
+    half_wells = []
+    for start in range(0, NX, 8):
+        x = 2 * (low_run ^ run_at(start % HALF_X)) + (core if start < HALF_X else 1 - core)
+        place_x = (x.astype(jnp.float32) - (NX - 1) / 2.0) / (NX / 2.0)
+        half_well = (0.5 * WELL) * (place_x * place_x + place_y * place_y)
+        half_wells.append(jnp.concatenate([half_well] * (width // 128), axis=1))
 
     def along_x(b):
         parts = [
@@ -193,12 +195,9 @@
         reals = []
         imags = []
         for start in range(0, NX, 8):
-            parity = core if start < HALF_X else 1 - core
-            x = 2 * (low_run ^ run_at(start % HALF_X)) + parity
-            place_x = (x.astype(jnp.float32) - (NX - 1) / 2.0) / (NX / 2.0)
-            real = first[start : start + 8] * scale
-            imag = first[NX + start : NX + start + 8] * scale
-            cos_turn, sin_turn = turns(KERR * (real * real + imag * imag) - (WELL * place_x * place_x + well_y))
+            real = first[start : start + 8]
+            imag = first[NX + start : NX + start + 8]
+            cos_turn, sin_turn = turns(half_kerr * (real * real + imag * imag) - half_wells[start // 8])
             reals.append(real * cos_turn - imag * sin_turn)
             imags.append(real * sin_turn + imag * cos_turn)
         return jnp.concatenate(reals + imags, axis=0)
@@ -216,7 +215,7 @@
     outs = along_t(blocks, t_table_ref)
     for p in range(2):
         for g in range(4):
-            out_ref[rows_of(g, p, 2), :] = outs[p][g]
+            out_ref[rows_of(g, p, 2), :] = outs[p][g] * scale
 
 
 def last_kernel(in_ref, table_ref, out_ref):

time: 65.8 us -> 65.7 us (level)
  no operation moved by 1% of the time
where the time goes in v7:
time: 65.7 us; the launch traced here: 65.4 us
  blocking collectives  56.3 us (86%)
  Pallas kernels  4.59 us (7%)
  starting transfers between devices  3.3 us (5%)
  waiting for transfers between devices  1.16 us (2%)
    all_to_all x2, blocking collectives, to_chips(): lax.all_to_all(rows.reshape(NY, 1, count * 128), DEVICES, split_axis=0, c...  56.3 us
    pallas_call x4, Pallas kernels, call(): pl.pallas_call(kernel, in_specs=[pl.BlockSpec(memory_space=source) for _...  4.59 us
    ppermute x1, starting transfers between devices, on_device(): other = lax.ppermute(mine, 'c', [(0, 1), (1, 0)])  3.3 us
  transfers between devices with their start and end apart: 1, of which 1 were waited for; matrix products, arithmetic and copies ran while one was open for 0% of the time, Pallas kernels for 0%

profile of v7, /device:TPU:1, one launch (start us, length us, event | category | flops | bytes accessed | tf_op | source)
XLA Modules:
  0.0 65.4 jit_solution(8344059100423890598)
XLA Ops:
  0.0 1.4 %first_kernel.1 = f32[768,128]{1,0:T(8,128)S(1)} custom-call(f32[2,256,128]{2,1,0:T(8,128)} %bitcast.12, bf16[2,256,256]{2,1,0:T(8,128)(2,1)} %constant.6.clone.table_hbm.table_ref), custom_call_target="tpu_custom_call" | custom-call | tf_op jit(solution)/shard_map/first_kernel/pallas_call | solution.py:233
  1.4 0.0 copy-start
  1.4 33.9 %all_to_all.10 = f32[256,1,384]{2,1,0:T(1,128)S(1)} all-to-all(f32[256,1,384]{2,1,0:T(1,128)S(1)} %bitcast.8), channel_id=1, replica_groups={{296,40,424,168,360,104,488,232,264,8,392,136,328,72,456,200,312,56,440..., dimensions={0} | all-to-all | bytes 786432 | tf_op jit(solution)/shard_map/all_to_all | solution.py:254
  35.3 0.0 copy-done
  35.3 0.0 copy-start.2
  35.3 0.6 time_kernel.1.mine_ref
  35.9 3.3 %collective-permute-start = (f32[136,512]{1,0:T(8,128)S(1)}, f32[136,512]{1,0:T(8,128)S(1)}, u32[]{:S(2)}, u32[]{:S(2)}) collective-permute-start(f32[136,512]{1,0:T(8,128)S(1)} %time_kernel.1.mine_ref), channel_id=1, source_target_pairs={{0,4},{4,0},{1,5},{5,1},{2,6},{6,2},{3,7},{7,3},{8,12},{12,8},{9,1... | collective-permute-start | bytes 835592 | tf_op jit(solution)/shard_map/ppermute | solution.py:270
  39.2 1.2 %collective-permute-done.other_ref = f32[136,512]{1,0:T(8,128)S(1)} collective-permute-done((f32[136,512]{1,0:T(8,128)S(1)}, f32[136,512]{1,0:T(8,128)S(1)}, u32[]{:S(2)}, u32[]{:S(2)}) %collective-permute-start) | collective-permute-done | bytes 278560 | tf_op jit(solution)/shard_map/ppermute | solution.py:270
  40.4 0.0 copy-done.2
  40.4 1.5 %kick_kernel.1 = f32[512,128]{1,0:T(8,128)S(1)} custom-call(f32[136,512]{1,0:T(8,128)S(1)} %time_kernel.1.mine_ref, f32[136,512]{1,0:T(8,128)S(1)} %collective-permute-done.other_ref, bf16[2,2,256,256]{3,2,1,0:T(8,128)(2,1)S(1)} %copy-done.2, bf16[2,256,512]{2,1,0:T(8,128)(2,1)S(1)} %copy-done), custom_call_target="tpu_custom_call" | custom-call | tf_op jit(solution)/shard_map/kick_kernel/pallas_call | solution.py:233
  41.9 0.0 copy-start.1
  41.9 22.4 %all_to_all.11 = f32[256,1,256]{2,1,0:T(1,128)S(1)} all-to-all(f32[256,1,256]{2,1,0:T(1,128)S(1)} %bitcast.10), channel_id=1, replica_groups={{296,40,424,168,360,104,488,232,264,8,392,136,328,72,456,200,312,56,440..., dimensions={0} | all-to-all | bytes 524288 | tf_op jit(solution)/shard_map/all_to_all | solution.py:254
  64.4 0.0 copy-done.1
  64.4 1.1 %last_kernel.1 = f32[2,256,128]{2,1,0:T(8,128)} custom-call(f32[512,128]{1,0:T(8,128)S(1)} %bitcast.11, bf16[2,256,256]{2,1,0:T(8,128)(2,1)S(1)} %copy-done.1), custom_call_target="tpu_custom_call" | custom-call | tf_op jit(solution)/shard_map/last_kernel/pallas_call | solution.py:233
Async XLA Ops:
  1.4 33.9 %copy-start = (bf16[2,256,512]{2,1,0:T(8,128)(2,1)S(1)}, bf16[2,256,512]{2,1,0:T(8,128)(2,1)}, u32[]{:S(2)}) copy-start(bf16[2,256,512]{2,1,0:T(8,128)(2,1)} %constant.7.clone.table_ref.t_table_ref) | copy-start | bytes 1572868
  35.3 5.1 %copy-start.2 = (bf16[2,2,256,256]{3,2,1,0:T(8,128)(2,1)S(1)}, bf16[2,2,256,256]{3,2,1,0:T(8,128)(2,1)}, u32[]{:S(2)}) copy-start(bf16[2,2,256,256]{3,2,1,0:T(8,128)(2,1)} %constant.8.clone.x_table_ref) | copy-start | bytes 1572868
  35.9 4.5 %collective-permute-start = (f32[136,512]{1,0:T(8,128)S(1)}, f32[136,512]{1,0:T(8,128)S(1)}, u32[]{:S(2)}, u32[]{:S(2)}) collective-permute-start(f32[136,512]{1,0:T(8,128)S(1)} %time_kernel.1.mine_ref), channel_id=1, source_target_pairs={{0,4},{4,0},{1,5},{5,1},{2,6},{6,2},{3,7},{7,3},{8,12},{12,8},{9,1... | collective-permute-start | bytes 835592 | tf_op jit(solution)/shard_map/ppermute | solution.py:270
  41.9 22.4 %copy-start.1 = (bf16[2,256,256]{2,1,0:T(8,128)(2,1)S(1)}, bf16[2,256,256]{2,1,0:T(8,128)(2,1)}, u32[]{:S(2)}) copy-start(bf16[2,256,256]{2,1,0:T(8,128)(2,1)} %constant.6.clone.table_hbm.table_ref) | copy-start | bytes 786436

commit v8 on v7

--- a/solution.py
+++ b/solution.py
@@ -153,21 +153,12 @@
     out_ref[pl.ds(2, NY, stride=3), :] = jnp.broadcast_to(power, (NY, 128))
 
 
-def time_kernel(in_ref, table_ref, out_ref):
-    blocks = [[in_ref[rows_of(g, p, 3), :] for g in range(4)] for p in range(2)]
-    outs = along_t(blocks, table_ref)
-    for p in range(2):
-        for g in range(4):
-            out_ref[p * HALF_X : (p + 1) * HALF_X, 128 * g : 128 * (g + 1)] = outs[p][g]
-    power = jnp.sum(in_ref[pl.ds(2, NY, stride=3), :], axis=0, keepdims=True)
-    out_ref[NX:, :128] = jnp.broadcast_to(power, (8, 128))
-
-
 def kick_kernel(mine_ref, other_ref, x_table_ref, t_table_ref, out_ref):
     core = lax.axis_index("c")
     position = position_of(lax.axis_index(("z", "x", "h")), lax.axis_index("t"))
     place_y = (position.astype(jnp.float32) - (NY - 1) / 2.0) / (NY / 2.0)
-    total = jnp.sum(mine_ref[NX : NX + 1, :128] + other_ref[NX : NX + 1, :128], axis=1, keepdims=True)
+    powers = mine_ref[pl.ds(2, NY, stride=3), :] + other_ref[pl.ds(2, NY, stride=3), :]
+    total = jnp.sum(jnp.sum(powers, axis=0, keepdims=True), axis=1, keepdims=True)
     scale = 1.0 / jnp.sqrt(total * (1.0 / (NX * NY * NT)) + EPSILON)
     table = x_table_ref[0, core]
     table_low = x_table_ref[1, core]
@@ -182,11 +173,16 @@
         half_well = (0.5 * WELL) * (place_x * place_x + place_y * place_y)
         half_wells.append(jnp.concatenate([half_well] * (width // 128), axis=1))
 
+    turned = []
+    for ref in (mine_ref, other_ref):
+        blocks = [[ref[rows_of(g, p, 3), :] for g in range(4)] for p in range(2)]
+        turned.append(along_t(blocks, t_table_ref))
+
     def along_x(b):
         parts = [
-            ref[p * HALF_X : (p + 1) * HALF_X, b * width : (b + 1) * width]
+            jnp.concatenate(outs[p][2 * b : 2 * b + 2], axis=1)
             for p in range(2)
-            for ref in (mine_ref, other_ref)
+            for outs in turned
         ]
         high, low = pieces(jnp.concatenate(parts, axis=0))
         return dot(table, high) + (dot(table, low) + dot(table_low, high))
@@ -266,7 +262,7 @@
     scratch = [pltpu.VMEM((2, NY, 128), jnp.float32), pltpu.VMEM(y_table.shape, jnp.bfloat16), pltpu.SemaphoreType.DMA((2,))]
     from_hbm = [pltpu.with_memory_space_constraint(a, pltpu.HBM) for a in (field.reshape(2, NY, 128), y_table)]
     rows = call(first_kernel, (3 * NY, 128), *from_hbm, scratch=scratch, direct=True)
-    mine = call(time_kernel, (NX + 8, NT), to_chips(rows, 3), t_table)
+    mine = to_chips(rows, 3)
     other = lax.ppermute(mine, "c", [(0, 1), (1, 0)])
     rows = call(kick_kernel, (2 * NY, 128), mine, other, x_table, t_table)
     out = call(last_kernel, (2, NY, 128), to_chips(rows, 2), y_table)

time: 65.7 us -> 67 us (1.020)
  Pallas kernels: 4.59 us -> 5.73 us
    pallas_call x4 -> x3, Pallas kernels: 4.59 us -> 5.73 us  [call(): pl.pallas_call(kernel, in_specs=[pl.BlockSpec(memory_space=source) for _...]
where the time goes in v8:
time: 67 us; the launch traced here: 66.7 us
  blocking collectives  56.3 us (84%)
  Pallas kernels  5.73 us (9%)
  starting transfers between devices  3.29 us (5%)
  waiting for transfers between devices  1.33 us (2%)
    all_to_all x2, blocking collectives, to_chips(): lax.all_to_all(rows.reshape(NY, 1, count * 128), DEVICES, split_axis=0, c...  56.3 us
    pallas_call x3, Pallas kernels, call(): pl.pallas_call(kernel, in_specs=[pl.BlockSpec(memory_space=source) for _...  5.73 us
    ppermute x1, starting transfers between devices, on_device(): other = lax.ppermute(mine, 'c', [(0, 1), (1, 0)])  3.29 us
  transfers between devices with their start and end apart: 1, of which 1 were waited for; matrix products, arithmetic and copies ran while one was open for 0% of the time, Pallas kernels for 0%

profile of v8, /device:TPU:1, one launch (start us, length us, event | category | flops | bytes accessed | tf_op | source)
XLA Modules:
  0.0 66.7 jit_solution(13092961959924861547)
XLA Ops:
  0.0 0.0 copy-start.2
  0.0 1.5 %first_kernel.1 = f32[768,128]{1,0:T(8,128)S(1)} custom-call(f32[2,256,128]{2,1,0:T(8,128)} %bitcast.13, bf16[2,256,256]{2,1,0:T(8,128)(2,1)} %constant.6.clone.table_hbm.table_ref), custom_call_target="tpu_custom_call" | custom-call | tf_op jit(solution)/shard_map/first_kernel/pallas_call | solution.py:229
  1.5 0.0 copy-start.1
  1.5 33.9 %all_to_all.10 = f32[256,1,384]{2,1,0:T(1,128)S(1)} all-to-all(f32[256,1,384]{2,1,0:T(1,128)S(1)} %bitcast.10), channel_id=1, replica_groups={{296,40,424,168,360,104,488,232,264,8,392,136,328,72,456,200,312,56,440..., dimensions={0} | all-to-all | bytes 786432 | tf_op jit(solution)/shard_map/all_to_all | solution.py:250
  35.4 3.3 %collective-permute-start = (f32[768,128]{1,0:T(8,128)S(1)}, f32[768,128]{1,0:T(8,128)S(1)}, u32[]{:S(2)}, u32[]{:S(2)}) collective-permute-start(f32[768,128]{1,0:T(8,128)S(1)} %bitcast.8), channel_id=1, source_target_pairs={{0,4},{4,0},{1,5},{5,1},{2,6},{6,2},{3,7},{7,3},{8,12},{12,8},{9,1... | collective-permute-start | bytes 1179656 | tf_op jit(solution)/shard_map/ppermute | solution.py:266
  38.7 1.3 %collective-permute-done.other_ref = f32[768,128]{1,0:T(8,128)S(1)} collective-permute-done((f32[768,128]{1,0:T(8,128)S(1)}, f32[768,128]{1,0:T(8,128)S(1)}, u32[]{:S(2)}, u32[]{:S(2)}) %collective-permute-start) | collective-permute-done | bytes 393248 | tf_op jit(solution)/shard_map/ppermute | solution.py:266
  40.0 0.0 copy-done.2
  40.0 0.0 copy-done.1
  40.0 3.2 %kick_kernel.1 = f32[512,128]{1,0:T(8,128)S(1)} custom-call(f32[768,128]{1,0:T(8,128)S(1)} %bitcast.9, f32[768,128]{1,0:T(8,128)S(1)} %collective-permute-done.other_ref, bf16[2,2,256,256]{3,2,1,0:T(8,128)(2,1)S(1)} %copy-done.1, bf16[2,256,512]{2,1,0:T(8,128)(2,1)S(1)} %copy-done.2), custom_call_target="tpu_custom_call" | custom-call | tf_op jit(solution)/shard_map/kick_kernel/pallas_call | solution.py:229
  43.2 0.0 copy-start
  43.2 22.4 %all_to_all.11 = f32[256,1,256]{2,1,0:T(1,128)S(1)} all-to-all(f32[256,1,256]{2,1,0:T(1,128)S(1)} %bitcast.12), channel_id=1, replica_groups={{296,40,424,168,360,104,488,232,264,8,392,136,328,72,456,200,312,56,440..., dimensions={0} | all-to-all | bytes 524288 | tf_op jit(solution)/shard_map/all_to_all | solution.py:250
  65.6 0.0 copy-done
  65.6 1.1 %last_kernel.1 = f32[2,256,128]{2,1,0:T(8,128)} custom-call(f32[512,128]{1,0:T(8,128)S(1)} %bitcast.11, bf16[2,256,256]{2,1,0:T(8,128)(2,1)S(1)} %copy-done), custom_call_target="tpu_custom_call" | custom-call | tf_op jit(solution)/shard_map/last_kernel/pallas_call | solution.py:229
Async XLA Ops:
  0.0 40.0 %copy-start.2 = (bf16[2,256,512]{2,1,0:T(8,128)(2,1)S(1)}, bf16[2,256,512]{2,1,0:T(8,128)(2,1)}, u32[]{:S(2)}) copy-start(bf16[2,256,512]{2,1,0:T(8,128)(2,1)} %constant.7.clone.t_table_ref) | copy-start | bytes 1572868
  1.5 38.5 %copy-start.1 = (bf16[2,2,256,256]{3,2,1,0:T(8,128)(2,1)S(1)}, bf16[2,2,256,256]{3,2,1,0:T(8,128)(2,1)}, u32[]{:S(2)}) copy-start(bf16[2,2,256,256]{3,2,1,0:T(8,128)(2,1)} %constant.8.clone.x_table_ref) | copy-start | bytes 1572868
  35.4 4.6 %collective-permute-start = (f32[768,128]{1,0:T(8,128)S(1)}, f32[768,128]{1,0:T(8,128)S(1)}, u32[]{:S(2)}, u32[]{:S(2)}) collective-permute-start(f32[768,128]{1,0:T(8,128)S(1)} %bitcast.8), channel_id=1, source_target_pairs={{0,4},{4,0},{1,5},{5,1},{2,6},{6,2},{3,7},{7,3},{8,12},{12,8},{9,1... | collective-permute-start | bytes 1179656 | tf_op jit(solution)/shard_map/ppermute | solution.py:266
  43.2 22.5 %copy-start = (bf16[2,256,256]{2,1,0:T(8,128)(2,1)S(1)}, bf16[2,256,256]{2,1,0:T(8,128)(2,1)}, u32[]{:S(2)}) copy-start(bf16[2,256,256]{2,1,0:T(8,128)(2,1)} %constant.6.clone.table_hbm.table_ref) | copy-start | bytes 786436

commit v9 on v7

--- a/solution.py
+++ b/solution.py
@@ -218,22 +218,29 @@
             out_ref[rows_of(g, p, 2), :] = outs[p][g] * scale
 
 
-def last_kernel(in_ref, table_ref, out_ref):
-    real = in_ref[pl.ds(0, NY, stride=2), :]
-    imag = in_ref[pl.ds(1, NY, stride=2), :]
-    reals, imags = along_y(real, imag, table_ref)
+def last_kernel(in_ref, table_ref, out_hbm, out_ref, sems):
     half = NY // 2
+    parts = [[in_ref[pl.ds(2 * half * j + p, half, stride=2), :] for p in range(2)] for j in range(2)]
+    halves = [pieces(jnp.concatenate(part, axis=1)) for part in parts]
+    copies = []
     for j in range(2):
-        out_ref[0, j * half : (j + 1) * half] = reals[j]
-        out_ref[1, j * half : (j + 1) * half] = imags[j]
-
-
-def call(kernel, shape, *args, scratch=(), direct=False):
+        high, low = [jnp.concatenate([halves[j][k], halves[1 - j][k]], axis=0) for k in range(2)]
+        r = dot(table_ref[0], high) + (dot(table_ref[0], low) + dot(table_ref[1], high))
+        rows = pl.ds(j * half, half)
+        out_ref[0, rows] = r[:half, :128] - r[half:, 128:]
+        out_ref[1, rows] = r[:half, 128:] + r[half:, :128]
+        copies.append(pltpu.make_async_copy(out_ref.at[:, rows], out_hbm.at[:, rows], sems.at[j]))
+        copies[j].start()
+    for copy in copies:
+        copy.wait()
+
+
+def call(kernel, shape, *args, scratch=(), direct=False, out_space=pltpu.VMEM):
     source = pltpu.HBM if direct else pltpu.VMEM
     return pl.pallas_call(
         kernel,
         in_specs=[pl.BlockSpec(memory_space=source) for _ in args],
-        out_specs=pl.BlockSpec(memory_space=pltpu.VMEM),
+        out_specs=pl.BlockSpec(memory_space=out_space),
         out_shape=jax.ShapeDtypeStruct(shape, jnp.float32),
         scratch_shapes=list(scratch),
         compiler_params=pltpu.CompilerParams(vmem_limit_bytes=16 * 2**20),
@@ -269,7 +276,8 @@
     mine = call(time_kernel, (NX + 8, NT), to_chips(rows, 3), t_table)
     other = lax.ppermute(mine, "c", [(0, 1), (1, 0)])
     rows = call(kick_kernel, (2 * NY, 128), mine, other, x_table, t_table)
-    out = call(last_kernel, (2, NY, 128), to_chips(rows, 2), y_table)
+    scratch = [pltpu.VMEM((2, NY, 128), jnp.float32), pltpu.SemaphoreType.DMA((2,))]
+    out = call(last_kernel, (2, NY, 128), to_chips(rows, 2), y_table, scratch=scratch, out_space=pltpu.HBM)
     return out.reshape(2, 1, NY, 128)
 
 

time: 65.7 us -> 65.7 us (level)
  no operation moved by 1% of the time
where the time goes in v9:
time: 65.7 us; the launch traced here: 65.4 us
  blocking collectives  56.3 us (86%)
  Pallas kernels  4.6 us (7%)
  starting transfers between devices  3.3 us (5%)
  waiting for transfers between devices  1.16 us (2%)
    all_to_all x2, blocking collectives, to_chips(): lax.all_to_all(rows.reshape(NY, 1, count * 128), DEVICES, split_axis=0, c...  56.3 us
    pallas_call x4, Pallas kernels, call(): pl.pallas_call(kernel, in_specs=[pl.BlockSpec(memory_space=source) for _...  4.6 us
    ppermute x1, starting transfers between devices, on_device(): other = lax.ppermute(mine, 'c', [(0, 1), (1, 0)])  3.3 us
  transfers between devices with their start and end apart: 1, of which 1 were waited for; matrix products, arithmetic and copies ran while one was open for 0% of the time, Pallas kernels for 0%

profile of v9, /device:TPU:1, one launch (start us, length us, event | category | flops | bytes accessed | tf_op | source)
XLA Modules:
  0.0 65.4 jit_solution(268328186179767126)
XLA Ops:
  0.0 1.4 %first_kernel.1 = f32[768,128]{1,0:T(8,128)S(1)} custom-call(f32[2,256,128]{2,1,0:T(8,128)} %bitcast.12, bf16[2,256,256]{2,1,0:T(8,128)(2,1)} %constant.6.clone.table_hbm.table_ref), custom_call_target="tpu_custom_call" | custom-call | tf_op jit(solution)/shard_map/first_kernel/pallas_call | solution.py:240
  1.4 0.0 copy-start
  1.4 33.9 %all_to_all.10 = f32[256,1,384]{2,1,0:T(1,128)S(1)} all-to-all(f32[256,1,384]{2,1,0:T(1,128)S(1)} %bitcast.8), channel_id=1, replica_groups={{296,40,424,168,360,104,488,232,264,8,392,136,328,72,456,200,312,56,440..., dimensions={0} | all-to-all | bytes 786432 | tf_op jit(solution)/shard_map/all_to_all | solution.py:261
  35.3 0.0 copy-done
  35.3 0.0 copy-start.2
  35.3 0.6 time_kernel.1.mine_ref
  35.9 3.3 %collective-permute-start = (f32[136,512]{1,0:T(8,128)S(1)}, f32[136,512]{1,0:T(8,128)S(1)}, u32[]{:S(2)}, u32[]{:S(2)}) collective-permute-start(f32[136,512]{1,0:T(8,128)S(1)} %time_kernel.1.mine_ref), channel_id=1, source_target_pairs={{0,4},{4,0},{1,5},{5,1},{2,6},{6,2},{3,7},{7,3},{8,12},{12,8},{9,1... | collective-permute-start | bytes 835592 | tf_op jit(solution)/shard_map/ppermute | solution.py:277
  39.2 1.2 %collective-permute-done.other_ref = f32[136,512]{1,0:T(8,128)S(1)} collective-permute-done((f32[136,512]{1,0:T(8,128)S(1)}, f32[136,512]{1,0:T(8,128)S(1)}, u32[]{:S(2)}, u32[]{:S(2)}) %collective-permute-start) | collective-permute-done | bytes 278560 | tf_op jit(solution)/shard_map/ppermute | solution.py:277
  40.4 0.0 copy-done.2
  40.4 1.5 %kick_kernel.1 = f32[512,128]{1,0:T(8,128)S(1)} custom-call(f32[136,512]{1,0:T(8,128)S(1)} %time_kernel.1.mine_ref, f32[136,512]{1,0:T(8,128)S(1)} %collective-permute-done.other_ref, bf16[2,2,256,256]{3,2,1,0:T(8,128)(2,1)S(1)} %copy-done.2, bf16[2,256,512]{2,1,0:T(8,128)(2,1)S(1)} %copy-done), custom_call_target="tpu_custom_call" | custom-call | tf_op jit(solution)/shard_map/kick_kernel/pallas_call | solution.py:240
  41.9 0.0 copy-start.1
  41.9 22.4 %all_to_all.11 = f32[256,1,256]{2,1,0:T(1,128)S(1)} all-to-all(f32[256,1,256]{2,1,0:T(1,128)S(1)} %bitcast.10), channel_id=1, replica_groups={{296,40,424,168,360,104,488,232,264,8,392,136,328,72,456,200,312,56,440..., dimensions={0} | all-to-all | bytes 524288 | tf_op jit(solution)/shard_map/all_to_all | solution.py:261
  64.4 0.0 copy-done.1
  64.4 1.1 %last_kernel.1 = f32[2,256,128]{2,1,0:T(8,128)} custom-call(f32[512,128]{1,0:T(8,128)S(1)} %bitcast.11, bf16[2,256,256]{2,1,0:T(8,128)(2,1)S(1)} %copy-done.1), custom_call_target="tpu_custom_call" | custom-call | tf_op jit(solution)/shard_map/last_kernel/pallas_call | solution.py:240
Async XLA Ops:
  1.4 33.9 %copy-start = (bf16[2,256,512]{2,1,0:T(8,128)(2,1)S(1)}, bf16[2,256,512]{2,1,0:T(8,128)(2,1)}, u32[]{:S(2)}) copy-start(bf16[2,256,512]{2,1,0:T(8,128)(2,1)} %constant.7.clone.table_ref.t_table_ref) | copy-start | bytes 1572868
  35.3 5.1 %copy-start.2 = (bf16[2,2,256,256]{3,2,1,0:T(8,128)(2,1)S(1)}, bf16[2,2,256,256]{3,2,1,0:T(8,128)(2,1)}, u32[]{:S(2)}) copy-start(bf16[2,2,256,256]{3,2,1,0:T(8,128)(2,1)} %constant.8.clone.x_table_ref) | copy-start | bytes 1572868
  35.9 4.5 %collective-permute-start = (f32[136,512]{1,0:T(8,128)S(1)}, f32[136,512]{1,0:T(8,128)S(1)}, u32[]{:S(2)}, u32[]{:S(2)}) collective-permute-start(f32[136,512]{1,0:T(8,128)S(1)} %time_kernel.1.mine_ref), channel_id=1, source_target_pairs={{0,4},{4,0},{1,5},{5,1},{2,6},{6,2},{3,7},{7,3},{8,12},{12,8},{9,1... | collective-permute-start | bytes 835592 | tf_op jit(solution)/shard_map/ppermute | solution.py:277
  41.9 22.4 %copy-start.1 = (bf16[2,256,256]{2,1,0:T(8,128)(2,1)S(1)}, bf16[2,256,256]{2,1,0:T(8,128)(2,1)}, u32[]{:S(2)}) copy-start(bf16[2,256,256]{2,1,0:T(8,128)(2,1)} %constant.6.clone.table_hbm.table_ref) | copy-start | bytes 786436

commit v10 on v7

--- a/solution.py
+++ b/solution.py
@@ -17,7 +17,7 @@
 SLAB = ("z", "x", "h", "c")
 DEVICES = ("z", "x", "h", "c", "t")
 RUN_BITS = (5, 4, 3, 2, 1, 0)
-FLIP = 37
+FLIP = 45
 T_HIGH = True
 
 TWO_PI = 2.0 * math.pi

time: 65.7 us -> 65.9 us (level)
  no operation moved by 1% of the time
where the time goes in v10:
time: 65.9 us; the launch traced here: 65.6 us
  blocking collectives  56.7 us (86%)
  Pallas kernels  4.59 us (7%)
  starting transfers between devices  3.09 us (5%)
  waiting for transfers between devices  1.16 us (2%)
    all_to_all x2, blocking collectives, to_chips(): lax.all_to_all(rows.reshape(NY, 1, count * 128), DEVICES, split_axis=0, c...  56.7 us
    pallas_call x4, Pallas kernels, call(): pl.pallas_call(kernel, in_specs=[pl.BlockSpec(memory_space=source) for _...  4.59 us
    ppermute x1, starting transfers between devices, on_device(): other = lax.ppermute(mine, 'c', [(0, 1), (1, 0)])  3.09 us
  transfers between devices with their start and end apart: 1, of which 1 were waited for; matrix products, arithmetic and copies ran while one was open for 0% of the time, Pallas kernels for 0%

profile of v10, /device:TPU:1, one launch (start us, length us, event | category | flops | bytes accessed | tf_op | source)
XLA Modules:
  0.0 65.6 jit_solution(1385343099256438443)
XLA Ops:
  0.0 1.4 %first_kernel.1 = f32[768,128]{1,0:T(8,128)S(1)} custom-call(f32[2,256,128]{2,1,0:T(8,128)} %bitcast.12, bf16[2,256,256]{2,1,0:T(8,128)(2,1)} %constant.6.clone.table_hbm.table_ref), custom_call_target="tpu_custom_call" | custom-call | tf_op jit(solution)/shard_map/first_kernel/pallas_call | solution.py:233
  1.4 0.0 copy-start
  1.4 33.7 %all_to_all.10 = f32[256,1,384]{2,1,0:T(1,128)S(1)} all-to-all(f32[256,1,384]{2,1,0:T(1,128)S(1)} %bitcast.8), channel_id=1, replica_groups={{360,104,488,232,296,40,424,168,328,72,456,200,264,8,392,136,376,120,50..., dimensions={0} | all-to-all | bytes 786432 | tf_op jit(solution)/shard_map/all_to_all | solution.py:254
  35.1 0.0 copy-done
  35.1 0.0 copy-start.2
  35.1 0.6 time_kernel.1.mine_ref
  35.7 3.1 %collective-permute-start = (f32[136,512]{1,0:T(8,128)S(1)}, f32[136,512]{1,0:T(8,128)S(1)}, u32[]{:S(2)}, u32[]{:S(2)}) collective-permute-start(f32[136,512]{1,0:T(8,128)S(1)} %time_kernel.1.mine_ref), channel_id=1, source_target_pairs={{0,4},{4,0},{1,5},{5,1},{2,6},{6,2},{3,7},{7,3},{8,12},{12,8},{9,1... | collective-permute-start | bytes 835592 | tf_op jit(solution)/shard_map/ppermute | solution.py:270
  38.8 1.2 %collective-permute-done.other_ref = f32[136,512]{1,0:T(8,128)S(1)} collective-permute-done((f32[136,512]{1,0:T(8,128)S(1)}, f32[136,512]{1,0:T(8,128)S(1)}, u32[]{:S(2)}, u32[]{:S(2)}) %collective-permute-start) | collective-permute-done | bytes 278560 | tf_op jit(solution)/shard_map/ppermute | solution.py:270
  40.0 0.0 copy-done.2
  40.0 1.5 %kick_kernel.1 = f32[512,128]{1,0:T(8,128)S(1)} custom-call(f32[136,512]{1,0:T(8,128)S(1)} %time_kernel.1.mine_ref, f32[136,512]{1,0:T(8,128)S(1)} %collective-permute-done.other_ref, bf16[2,2,256,256]{3,2,1,0:T(8,128)(2,1)S(1)} %copy-done.2, bf16[2,256,512]{2,1,0:T(8,128)(2,1)S(1)} %copy-done), custom_call_target="tpu_custom_call" | custom-call | tf_op jit(solution)/shard_map/kick_kernel/pallas_call | solution.py:233
  41.5 0.0 copy-start.1
  41.5 23.1 %all_to_all.11 = f32[256,1,256]{2,1,0:T(1,128)S(1)} all-to-all(f32[256,1,256]{2,1,0:T(1,128)S(1)} %bitcast.10), channel_id=1, replica_groups={{360,104,488,232,296,40,424,168,328,72,456,200,264,8,392,136,376,120,50..., dimensions={0} | all-to-all | bytes 524288 | tf_op jit(solution)/shard_map/all_to_all | solution.py:254
  64.5 0.0 copy-done.1
  64.5 1.1 %last_kernel.1 = f32[2,256,128]{2,1,0:T(8,128)} custom-call(f32[512,128]{1,0:T(8,128)S(1)} %bitcast.11, bf16[2,256,256]{2,1,0:T(8,128)(2,1)S(1)} %copy-done.1), custom_call_target="tpu_custom_call" | custom-call | tf_op jit(solution)/shard_map/last_kernel/pallas_call | solution.py:233
Async XLA Ops:
  1.4 33.7 %copy-start = (bf16[2,256,512]{2,1,0:T(8,128)(2,1)S(1)}, bf16[2,256,512]{2,1,0:T(8,128)(2,1)}, u32[]{:S(2)}) copy-start(bf16[2,256,512]{2,1,0:T(8,128)(2,1)} %constant.7.clone.table_ref.t_table_ref) | copy-start | bytes 1572868
  35.1 4.8 %copy-start.2 = (bf16[2,2,256,256]{3,2,1,0:T(8,128)(2,1)S(1)}, bf16[2,2,256,256]{3,2,1,0:T(8,128)(2,1)}, u32[]{:S(2)}) copy-start(bf16[2,2,256,256]{3,2,1,0:T(8,128)(2,1)} %constant.8.clone.x_table_ref) | copy-start | bytes 1572868
  35.7 4.3 %collective-permute-start = (f32[136,512]{1,0:T(8,128)S(1)}, f32[136,512]{1,0:T(8,128)S(1)}, u32[]{:S(2)}, u32[]{:S(2)}) collective-permute-start(f32[136,512]{1,0:T(8,128)S(1)} %time_kernel.1.mine_ref), channel_id=1, source_target_pairs={{0,4},{4,0},{1,5},{5,1},{2,6},{6,2},{3,7},{7,3},{8,12},{12,8},{9,1... | collective-permute-start | bytes 835592 | tf_op jit(solution)/shard_map/ppermute | solution.py:270
  41.5 23.1 %copy-start.1 = (bf16[2,256,256]{2,1,0:T(8,128)(2,1)S(1)}, bf16[2,256,256]{2,1,0:T(8,128)(2,1)}, u32[]{:S(2)}) copy-start(bf16[2,256,256]{2,1,0:T(8,128)(2,1)} %constant.6.clone.table_hbm.table_ref) | copy-start | bytes 786436

commit v11 on v7

--- a/solution.py
+++ b/solution.py
@@ -120,7 +120,7 @@
 
 
 def turns(half):
-    count = jnp.floor(half * (1.0 / math.pi) + 0.5)
+    count = jnp.round(half * (1.0 / math.pi))
     rest = ((half - count * 3.140625) - count * 9.67502593994140625e-4) - count * 1.509957990978376432e-7
     square = rest * rest
     sine = rest + (rest * square) * (

time: 65.7 us -> 65.7 us (level)
  no operation moved by 1% of the time
where the time goes in v11:
time: 65.7 us; the launch traced here: 65.4 us
  blocking collectives  56.3 us (86%)
  Pallas kernels  4.57 us (7%)
  starting transfers between devices  3.3 us (5%)
  waiting for transfers between devices  1.16 us (2%)
    all_to_all x2, blocking collectives, to_chips(): lax.all_to_all(rows.reshape(NY, 1, count * 128), DEVICES, split_axis=0, c...  56.3 us
    pallas_call x4, Pallas kernels, call(): pl.pallas_call(kernel, in_specs=[pl.BlockSpec(memory_space=source) for _...  4.57 us
    ppermute x1, starting transfers between devices, on_device(): other = lax.ppermute(mine, 'c', [(0, 1), (1, 0)])  3.3 us
  transfers between devices with their start and end apart: 1, of which 1 were waited for; matrix products, arithmetic and copies ran while one was open for 0% of the time, Pallas kernels for 0%

profile of v11, /device:TPU:1, one launch (start us, length us, event | category | flops | bytes accessed | tf_op | source)
XLA Modules:
  0.0 65.4 jit_solution(11611015984487773629)
XLA Ops:
  0.0 1.4 %first_kernel.1 = f32[768,128]{1,0:T(8,128)S(1)} custom-call(f32[2,256,128]{2,1,0:T(8,128)} %bitcast.12, bf16[2,256,256]{2,1,0:T(8,128)(2,1)} %constant.6.clone.table_hbm.table_ref), custom_call_target="tpu_custom_call" | custom-call | tf_op jit(solution)/shard_map/first_kernel/pallas_call | solution.py:233
  1.4 0.0 copy-start
  1.4 33.9 %all_to_all.10 = f32[256,1,384]{2,1,0:T(1,128)S(1)} all-to-all(f32[256,1,384]{2,1,0:T(1,128)S(1)} %bitcast.8), channel_id=1, replica_groups={{296,40,424,168,360,104,488,232,264,8,392,136,328,72,456,200,312,56,440..., dimensions={0} | all-to-all | bytes 786432 | tf_op jit(solution)/shard_map/all_to_all | solution.py:254
  35.3 0.0 copy-done
  35.3 0.0 copy-start.2
  35.3 0.6 time_kernel.1.mine_ref
  35.9 3.3 %collective-permute-start = (f32[136,512]{1,0:T(8,128)S(1)}, f32[136,512]{1,0:T(8,128)S(1)}, u32[]{:S(2)}, u32[]{:S(2)}) collective-permute-start(f32[136,512]{1,0:T(8,128)S(1)} %time_kernel.1.mine_ref), channel_id=1, source_target_pairs={{0,4},{4,0},{1,5},{5,1},{2,6},{6,2},{3,7},{7,3},{8,12},{12,8},{9,1... | collective-permute-start | bytes 835592 | tf_op jit(solution)/shard_map/ppermute | solution.py:270
  39.2 1.2 %collective-permute-done.other_ref = f32[136,512]{1,0:T(8,128)S(1)} collective-permute-done((f32[136,512]{1,0:T(8,128)S(1)}, f32[136,512]{1,0:T(8,128)S(1)}, u32[]{:S(2)}, u32[]{:S(2)}) %collective-permute-start) | collective-permute-done | bytes 278560 | tf_op jit(solution)/shard_map/ppermute | solution.py:270
  40.4 0.0 copy-done.2
  40.4 1.5 %kick_kernel.1 = f32[512,128]{1,0:T(8,128)S(1)} custom-call(f32[136,512]{1,0:T(8,128)S(1)} %time_kernel.1.mine_ref, f32[136,512]{1,0:T(8,128)S(1)} %collective-permute-done.other_ref, bf16[2,2,256,256]{3,2,1,0:T(8,128)(2,1)S(1)} %copy-done.2, bf16[2,256,512]{2,1,0:T(8,128)(2,1)S(1)} %copy-done), custom_call_target="tpu_custom_call" | custom-call | tf_op jit(solution)/shard_map/kick_kernel/pallas_call | solution.py:233
  41.9 0.0 copy-start.1
  41.9 22.5 %all_to_all.11 = f32[256,1,256]{2,1,0:T(1,128)S(1)} all-to-all(f32[256,1,256]{2,1,0:T(1,128)S(1)} %bitcast.10), channel_id=1, replica_groups={{296,40,424,168,360,104,488,232,264,8,392,136,328,72,456,200,312,56,440..., dimensions={0} | all-to-all | bytes 524288 | tf_op jit(solution)/shard_map/all_to_all | solution.py:254
  64.4 0.0 copy-done.1
  64.4 1.1 %last_kernel.1 = f32[2,256,128]{2,1,0:T(8,128)} custom-call(f32[512,128]{1,0:T(8,128)S(1)} %bitcast.11, bf16[2,256,256]{2,1,0:T(8,128)(2,1)S(1)} %copy-done.1), custom_call_target="tpu_custom_call" | custom-call | tf_op jit(solution)/shard_map/last_kernel/pallas_call | solution.py:233
Async XLA Ops:
  1.4 33.9 %copy-start = (bf16[2,256,512]{2,1,0:T(8,128)(2,1)S(1)}, bf16[2,256,512]{2,1,0:T(8,128)(2,1)}, u32[]{:S(2)}) copy-start(bf16[2,256,512]{2,1,0:T(8,128)(2,1)} %constant.7.clone.table_ref.t_table_ref) | copy-start | bytes 1572868
  35.3 5.1 %copy-start.2 = (bf16[2,2,256,256]{3,2,1,0:T(8,128)(2,1)S(1)}, bf16[2,2,256,256]{3,2,1,0:T(8,128)(2,1)}, u32[]{:S(2)}) copy-start(bf16[2,2,256,256]{3,2,1,0:T(8,128)(2,1)} %constant.8.clone.x_table_ref) | copy-start | bytes 1572868
  35.9 4.5 %collective-permute-start = (f32[136,512]{1,0:T(8,128)S(1)}, f32[136,512]{1,0:T(8,128)S(1)}, u32[]{:S(2)}, u32[]{:S(2)}) collective-permute-start(f32[136,512]{1,0:T(8,128)S(1)} %time_kernel.1.mine_ref), channel_id=1, source_target_pairs={{0,4},{4,0},{1,5},{5,1},{2,6},{6,2},{3,7},{7,3},{8,12},{12,8},{9,1... | collective-permute-start | bytes 835592 | tf_op jit(solution)/shard_map/ppermute | solution.py:270
  41.9 22.5 %copy-start.1 = (bf16[2,256,256]{2,1,0:T(8,128)(2,1)S(1)}, bf16[2,256,256]{2,1,0:T(8,128)(2,1)}, u32[]{:S(2)}) copy-start(bf16[2,256,256]{2,1,0:T(8,128)(2,1)} %constant.6.clone.table_hbm.table_ref) | copy-start | bytes 786436
